TPU v7x, 128 devices: a whole 4x4x4 slice. The times are simulated.
128 devices in a mesh: tm: 2 (over z_hi), seq: 64 (over y, z_lo, x, core).
Axes of the slice: x: 4, y: 4, z: 4 (z_hi: 2, z_lo: 2; z = z_hi * 2 + z_lo), core: 2. Of those that a mesh axis runs over, the one named last changes fastest.
Arguments:
- tokens: bfloat16 [2048, 5120], P(('tm', 'seq')), may hold values from -6 to 6
- w_query: bfloat16 [5120, 4096], P('seq'), may hold values from -0.078125 to 0.078125
- w_out: bfloat16 [4096, 5120], P(None, 'seq'), may hold values from -0.25 to 0.25
- k_cache: bfloat16 [16384, 4096], P(('tm', 'seq')), may hold values from -800 to 800
- v_cache: bfloat16 [16384, 4096], P(('tm', 'seq')), may hold values from -6 to 6
- radial_mask: int32 [16, 8, 128], replicated, may hold values from 0 to 1, as said below
- slot_frame: int32 [16], replicated, may hold values from 0 to 15, each once
Outputs:
- mixed: bfloat16 [2048, 5120], P(('tm', 'seq'))
Inputs may be any that keep to these rules, and one draw needn't show every extreme that they name: radial_mask[f, b, f * 8 + b] = 1 for every frame f and tile b. `slot_frame`: each of the 16 frames is held by exactly one slot.
All inputs are finite; a program needn't handle non-finite values.
Results may differ from a plain program's by a relative error of at most 0.012.
The roundings to bfloat16 on the way count: a program that leaves them out, or rounds other values in their place, can miss the bound.
Values may be sent and summed in bfloat16 or wider, within the bound.
No kernel may reach another device: no remote copies, remote signals or barrier semaphores. Data moves between devices by JAX's collectives and lax.ppermute only.
A program may use at most 128 MiB of HBM per device.

v0:
```python
import jax
import jax.numpy as jnp
from jax import lax
from jax.sharding import PartitionSpec as P

D = 5120
HD = 128
HEADS = 32
FRAMES = 16
BLOCK = 128
Q_DEV = 16


NEG = -1e30


def spread_columns(table, blocks, copies, groups):
    rows = table.shape[0]
    head_width = table.shape[1] // blocks
    grouped = table.reshape(rows, 1, blocks, 1, head_width)
    spread = jnp.broadcast_to(grouped, (rows, groups, blocks, copies, head_width))
    return spread.reshape(rows, groups * blocks * copies, head_width)


def on_device(tokens, w_query, w_out, k_cache, v_cache, radial_mask, slot_frame):
    seq_count = lax.axis_size("seq")
    group_count = lax.axis_size("tm")
    copies = max(1, seq_count // HEADS)
    per_dev = HEADS * copies // seq_count
    head_width = per_dev * HD
    blocks = seq_count // copies
    part_rows = Q_DEV // copies
    query_rows = part_rows * seq_count
    frame_tok = Q_DEV * seq_count
    frame_blocks = frame_tok // BLOCK
    per_group = FRAMES // group_count
    key_tile = 4 * BLOCK
    score_scale = HD ** (-0.5)
    my_seq = lax.axis_index("seq")
    my_group = lax.axis_index("tm")
    my_part = my_seq % copies
    split_rows = (
        tokens.reshape(copies, part_rows, D).transpose(1, 0, 2).reshape(part_rows, 1, copies, D)
    )
    token_send = jnp.broadcast_to(split_rows, (part_rows, blocks, copies, D)).reshape(
        part_rows, seq_count, D
    )
    query_send = spread_columns(w_query, blocks, copies, 1)
    frame = lax.dynamic_index_in_dim(slot_frame, my_group * per_group, 0, keepdims=False)
    onehot = (slot_frame[:, None] == lax.iota(jnp.int32, FRAMES)[None, :]).astype(jnp.float32)
    chosen = lax.dynamic_index_in_dim(radial_mask, frame, 0, keepdims=False).astype(jnp.float32)
    chosen = chosen.reshape(frame_blocks, FRAMES, frame_blocks)
    mask_slots = jnp.einsum("sf,qfb->qsb", onehot, chosen).reshape(
        frame_blocks, FRAMES * frame_blocks
    )
    row_index = lax.iota(jnp.int32, query_rows)
    token_index = row_index // part_rows * Q_DEV + my_part * part_rows + row_index % part_rows
    row_block = (token_index // BLOCK)[:, None] == lax.iota(jnp.int32, frame_blocks)[None, :]
    row_allowed = jnp.dot(
        row_block.astype(jnp.float32), mask_slots, preferred_element_type=jnp.float32
    )
    key_send = spread_columns(k_cache, blocks, copies, 1)
    value_send = spread_columns(v_cache, blocks, copies, 1)
    token_got, query_got, key_got, value_got = (
        lax.all_to_all(token_send, "seq", split_axis=1, concat_axis=0, tiled=True),
        lax.all_to_all(query_send, "seq", split_axis=1, concat_axis=0, tiled=True),
        lax.all_to_all(key_send, "seq", split_axis=1, concat_axis=0, tiled=True),
        lax.all_to_all(value_send, "seq", split_axis=1, concat_axis=0, tiled=True),
    )
    query = jnp.dot(
        token_got.reshape(query_rows, D),
        query_got.reshape(D, head_width),
        preferred_element_type=jnp.float32,
    )
    query = query.astype(jnp.bfloat16).reshape(query_rows, per_dev, HD)
    start_state = (
        jnp.full((query_rows, per_dev), NEG, jnp.float32),
        jnp.zeros((query_rows, per_dev), jnp.float32),
        jnp.zeros((query_rows, per_dev, HD), jnp.float32),
    )
    group_keys = key_got.reshape(-1, head_width)
    group_values = value_got.reshape(-1, head_width)
    keys = lax.all_gather(group_keys, "tm", axis=0, tiled=True)
    values = lax.all_gather(group_values, "tm", axis=0, tiled=True)
    tiles = keys.shape[0] // key_tile

    def one_tile(index, state):
        highest, denom, summed = state
        k_tile = lax.dynamic_slice_in_dim(keys, index * key_tile, key_tile, 0).reshape(
            key_tile, per_dev, HD
        )
        v_tile = lax.dynamic_slice_in_dim(values, index * key_tile, key_tile, 0).reshape(
            key_tile, per_dev, HD
        )
        first_block = index * key_tile // BLOCK
        allowed = lax.dynamic_slice_in_dim(row_allowed, first_block, key_tile // BLOCK, 1)
        keep = jnp.repeat(allowed > 0.5, BLOCK, axis=1)[:, None, :]
        scores = (
            jnp.einsum("qhd,khd->qhk", query, k_tile, preferred_element_type=jnp.float32)
            * score_scale
        )
        scores = jnp.where(keep, scores, NEG)
        new_high = jnp.maximum(highest, jnp.max(scores, axis=2))
        weights = jnp.where(keep, jnp.exp(scores - new_high[..., None]), 0.0)
        fade = jnp.exp(highest - new_high)
        denom = denom * fade + jnp.sum(weights, axis=2)
        update = jnp.einsum(
            "qhk,khd->qhd", weights.astype(jnp.bfloat16), v_tile, preferred_element_type=jnp.float32
        )
        summed = summed * fade[..., None] + update
        return (new_high, denom, summed)

    final_state = lax.fori_loop(0, tiles, one_tile, start_state)
    attended = (
        (final_state[2] / final_state[1][..., None])
        .astype(jnp.bfloat16)
        .reshape(query_rows, head_width)
    )
    out_columns = w_out.shape[1]
    out_send = jnp.broadcast_to(
        w_out.reshape(blocks, 1, head_width, out_columns), (blocks, copies, head_width, out_columns)
    )
    out_send = out_send.reshape(seq_count, head_width, out_columns)
    w_rows = lax.all_to_all(out_send, "seq", split_axis=0, concat_axis=2, tiled=True).reshape(
        head_width, D
    )
    part_pick = (
        (lax.iota(jnp.int32, copies) == my_part).astype(jnp.float32).reshape(1, copies, 1, 1)
    )
    sources = lax.axis_size("seq") * Q_DEV // Q_DEV
    partial_value = jnp.dot(attended, w_rows, preferred_element_type=jnp.float32).reshape(
        sources, 1, part_rows, D
    )
    return lax.psum_scatter(
        (partial_value * part_pick).reshape(lax.axis_size("seq") * Q_DEV, D),
        "seq",
        scatter_dimension=0,
        tiled=True,
    ).astype(jnp.bfloat16)


def solution(mesh):
    return jax.shard_map(
        on_device,
        mesh=mesh,
        in_specs=(
            P(("tm", "seq"), None),
            P("seq", None),
            P(None, "seq"),
            P(("tm", "seq"), None),
            P(("tm", "seq"), None),
            P(),
            P(),
        ),
        out_specs=P(("tm", "seq"), None),
        check_vma=False,
    )
```

profile of v0, /device:TPU:0, one launch (start us, length us, event | category | flops | bytes accessed | tf_op | source)
XLA Modules:
  0.0 712.9 jit_solution(3504346933268014614)
XLA Ops:
  6.5 1.2 copy-done
  8.1 1.9 broadcast_in_dim.94
  9.9 9.4 %all-to-all-start = ((bf16[128,64,128]{2,0,1:T(8,128)(2,1)}), bf16[128,64,128]{2,0,1:T(8,128)(2,1)S(1)}, u32[]{:S(2)}, u32[]{:S(2)}) async-start(bf16[128,64,128]{2,0,1:T(8,128)(2,1)} %bitcast.141), calls=%async_computation | async-start | bytes 4194304 | tf_op jit(solution)/shard_map/all_to_all | solution.py:67
  20.5 27.8 %all-to-all-done = bf16[128,64,128]{2,0,1:T(8,128)(2,1)S(1)} async-done(((bf16[128,64,128]{2,0,1:T(8,128)(2,1)}), bf16[128,64,128]{2,0,1:T(8,128)(2,1)S(1)}, u32[]{:S(2)}, u32[]{:S(2)}) %all-to-all-start) | async-done | bytes 2097184 | tf_op jit(solution)/shard_map/all_to_all | solution.py:67
  48.3 1.4 broadcast_in_dim.98
  49.7 5.5 all-to-all-start.2
  55.9 1.5 copy_bitcast_fusion
  57.5 18.3 %all-to-all-done.2 = bf16[80,64,128]{2,0,1:T(8,128)(2,1)} async-done(((bf16[80,64,128]{2,0,1:T(8,128)(2,1)}), bf16[80,64,128]{2,0,1:T(8,128)(2,1)}, u32[]{:S(2)}, u32[]{:S(2)}) %all-to-all-start.2) | async-done | bytes 1310752 | tf_op jit(solution)/shard_map/all_to_all | solution.py:66
  76.3 33.8 %all_to_all.75 = bf16[128,64,128]{2,0,1:T(8,128)(2,1)} all-to-all(bf16[128,64,128]{2,0,1:T(8,128)(2,1)S(1)} %bitcast.142), channel_id=1, replica_groups=mesh['tm'=2,'seq'=64] {'seq'}, dimensions={1} | all-to-all | bytes 4194304 | tf_op jit(solution)/shard_map/all_to_all | solution.py:68
  110.1 3.0 broadcast_in_dim.96
  113.0 5.8 all-to-all-start.1
  124.3 57.3 %all-to-all-done.1 = bf16[8,64,5120]{2,0,1:T(8,128)(2,1)} async-done(((bf16[8,64,5120]{2,0,1:T(8,128)(2,1)}), bf16[8,64,5120]{2,0,1:T(8,128)(2,1)}, u32[]{:S(2)}, u32[]{:S(2)}) %all-to-all-start.1) | async-done | bytes 5242912 | tf_op jit(solution)/shard_map/all_to_all | solution.py:65
  181.6 1.3 broadcast_in_dim.104
  182.9 7.5 %all-to-all-start.4 = ((bf16[64,128,80]{1,2,0:T(8,128)(2,1)}), bf16[64,128,80]{1,2,0:T(8,128)(2,1)S(1)}, u32[]{:S(2)}, u32[]{:S(2)}) async-start(bf16[64,128,80]{1,2,0:T(8,128)(2,1)} %bitcast.144), calls=%async_computation.4 | async-start | bytes 2621440 | tf_op jit(solution)/shard_map/all_to_all | solution.py:124
  190.5 4.4 fusion.19
  194.9 19.1 %all-gather.3.cloned.1.call-done = bf16[16384,128]{1,0:T(8,128)(2,1)} async-done(((bf16[8192,128]{1,0:T(8,128)(2,1)}), bf16[16384,128]{1,0:T(8,128)(2,1)}) %all-gather.3.cloned.1.call-update) | async-done | bytes 4194320 | tf_op jit(solution)/shard_map/all_gather | solution.py:83
  214.0 61.0 %all-gather.5.cloned.1.call-done = bf16[16384,128]{1,0:T(8,128)(2,1)} async-done(((bf16[8192,128]{1,0:T(8,128)(2,1)}), bf16[16384,128]{1,0:T(8,128)(2,1)}) %all-gather.5.cloned.1.call-update) | async-done | bytes 4194320 | tf_op jit(solution)/shard_map/all_gather | solution.py:84
  275.0 99.9 %while.20 = (s32[]{:T(128)}, f32[512,1]{0,1:T(1,128)S(1)}, f32[512,1]{0,1:T(1,128)S(1)}, f32[512,1,128]{0,2,1:T(8,128)S(1)}, f32[512,128]{0,1:T(8,128)S(1)}, /*i...) while((s32[]{:T(128)}, f32[512,1]{0,1:T(1,128)S(1)}, ...), condition=%wide.region_3.4_spmd.clone, body=%wide.region_0.3_spmd.clone.sunk | while | flops 136516096 | bytes 5941650 | solution.py:113
  278.2 1.2 fusion.64
  281.3 1.2 fusion.64
  284.4 1.2 fusion.64
  287.6 1.2 fusion.64
  290.7 1.2 fusion.64
  293.8 1.2 fusion.64
  296.9 1.2 fusion.64
  300.0 1.2 fusion.64
  303.2 1.2 fusion.64
  306.3 1.2 fusion.64
  309.4 1.2 fusion.64
  312.5 1.2 fusion.64
  315.7 1.2 fusion.64
  318.8 1.2 fusion.64
  321.9 1.2 fusion.64
  325.0 1.2 fusion.64
  328.2 1.2 fusion.64
  331.3 1.2 fusion.64
  334.4 1.2 fusion.64
  337.5 1.2 fusion.64
  340.7 1.2 fusion.64
  343.8 1.2 fusion.64
  350.0 1.2 fusion.64
  356.3 1.2 fusion.64
  362.5 1.2 fusion.64
  368.8 1.2 fusion.64
  375.0 1.6 fusion.23
  376.6 7.3 %bitcast_multiply_fusion = f32[1024,5120]{1,0:T(8,128)} fusion(f32[1024]{0:T(1024)S(1)} %mul.109, f32[64,8,5120]{2,1,0:T(8,128)S(1)} %fusion.23), kind=kLoop, calls=%fused_computation.23 | loop fusion | flops 5242880 | bytes 31461376 | tf_op jit(solution)/shard_map/mul | solution.py:135
  384.0 320.8 %reduce-scatter.2.cloned.1.call-done = f32[16,5120]{1,0:T(8,128)} async-done(((f32[1024,5120]{1,0:T(8,128)}), f32[16,5120]{1,0:T(8,128)}) %reduce-scatter.2.cloned.1.call-update) | async-done | bytes 327696 | tf_op jit(solution)/shard_map/reduce_scatter | solution.py:134
  704.8 1.7 convert_element_type.40
  (299 shorter events, 72.0 us)
Async XLA Ops:
  6.5 1.2 copy-start
  9.9 38.4 %all-to-all-start = ((bf16[128,64,128]{2,0,1:T(8,128)(2,1)}), bf16[128,64,128]{2,0,1:T(8,128)(2,1)S(1)}, u32[]{:S(2)}, u32[]{:S(2)}) async-start(bf16[128,64,128]{2,0,1:T(8,128)(2,1)} %bitcast.141), calls=%async_computation | async-start | bytes 4194304 | tf_op jit(solution)/shard_map/all_to_all | solution.py:67
  48.3 7.0 copy-start.2
  49.7 26.1 %all-to-all-start.2 = ((bf16[80,64,128]{2,0,1:T(8,128)(2,1)}), bf16[80,64,128]{2,0,1:T(8,128)(2,1)}, u32[]{:S(2)}, u32[]{:S(2)}) async-start(bf16[80,64,128]{2,0,1:T(8,128)(2,1)} %bitcast.145), calls=%async_computation.2 | async-start | bytes 2621440 | tf_op jit(solution)/shard_map/all_to_all | solution.py:66
  55.2 158.8 %all-gather.3.cloned.1.call-start = ((), (), s32[]{:S(2)}) async-start(), calls=%async_computation.6 | async-start | bytes 6291456 | tf_op jit(solution)/shard_map/all_gather | solution.py:83
  57.5 52.6 %copy-start.4 = (bf16[16,5120]{1,0:T(8,128)(2,1)S(1)}, bf16[16,5120]{1,0:T(8,128)(2,1)}, u32[]{:S(2)}) copy-start(bf16[16,5120]{1,0:T(8,128)(2,1)} %param.9) | copy-start | bytes 491524
  113.0 6.6 copy-start.5
  113.0 11.1 %copy-start.3 = (bf16[4096,80]{0,1:T(8,128)(2,1)S(1)}, bf16[4096,80]{0,1:T(8,128)(2,1)}, u32[]{:S(2)}) copy-start(bf16[4096,80]{0,1:T(8,128)(2,1)} %param.11) | copy-start | bytes 1966084
  113.0 68.5 %all-to-all-start.1 = ((bf16[8,64,5120]{2,0,1:T(8,128)(2,1)}), bf16[8,64,5120]{2,0,1:T(8,128)(2,1)}, u32[]{:S(2)}, u32[]{:S(2)}) async-start(bf16[8,64,5120]{2,0,1:T(8,128)(2,1)} %bitcast.138), calls=%async_computation.1 | async-start | bytes 10485760 | tf_op jit(solution)/shard_map/all_to_all | solution.py:65
  118.9 156.1 %all-gather.5.cloned.1.call-start = ((), (), s32[]{:S(2)}) async-start(), calls=%async_computation.7 | async-start | bytes 6291456 | tf_op jit(solution)/shard_map/all_gather | solution.py:84
  182.9 192.2 %all-to-all-start.4 = ((bf16[64,128,80]{1,2,0:T(8,128)(2,1)}), bf16[64,128,80]{1,2,0:T(8,128)(2,1)S(1)}, u32[]{:S(2)}, u32[]{:S(2)}) async-start(bf16[64,128,80]{1,2,0:T(8,128)(2,1)} %bitcast.144), calls=%async_computation.4 | async-start | bytes 2621440 | tf_op jit(solution)/shard_map/all_to_all | solution.py:124
  190.4 514.3 %reduce-scatter.2.cloned.1.call-start = ((), (), s32[]{:S(2)}) async-start(), calls=%async_computation.8 | async-start | bytes 21299200 | tf_op jit(solution)/shard_map/reduce_scatter | solution.py:134
  384.0 322.4 %copy-start.1 = (bf16[128,4096]{1,0:T(8,128)(2,1)S(1)}, bf16[128,4096]{1,0:T(8,128)(2,1)}, u32[]{:S(2)}) copy-start(bf16[128,4096]{1,0:T(8,128)(2,1)} %param.12) | copy-start | bytes 3145732
Sparse Core Ops, SparseCore 0:
  57.7 156.2 all-gather.2
  215.7 59.2 all-gather.4
  384.1 320.6 reduce-scatter.1
where the time goes:
time: 715 us; the launch traced here: 713 us
  waiting for transfers between devices  506 us (71%)
  matrix products  82.5 us (12%)
  blocking collectives  33.8 us (5%)
  other arithmetic  28.5 us (4%)
  starting transfers between devices  28.4 us (4%)
  local copies, waits for them, and re-layouts  16.1 us (2%)
  between operations  15.4 us (2%)
    reduce_scatter x1, waiting for transfers between devices, on_device(): lax.psum_scatter((partial_value * part_pick).reshape(lax.axis_size('seq')...  321 us
    all_gather x1, waiting for transfers between devices, on_device(): values = lax.all_gather(group_values, 'tm', axis=0, tiled=True)  61 us
    all_to_all x1, waiting for transfers between devices, on_device(): lax.all_to_all(token_send, 'seq', split_axis=1, concat_axis=0, tiled=True)  57.3 us
    dot_general x32, matrix products, one_tile(): jnp.einsum('qhd,khd->qhk', query, k_tile, preferred_element_type=jnp.floa...  38.6 us
    dot_general x32, matrix products, one_tile(): jnp.einsum('qhk,khd->qhd', weights.astype(jnp.bfloat16), v_tile, preferre...  37.4 us
    all_to_all x1, blocking collectives, on_device(): lax.all_to_all(value_send, 'seq', split_axis=1, concat_axis=0, tiled=True)  33.8 us
    all_to_all x1, waiting for transfers between devices, on_device(): lax.all_to_all(key_send, 'seq', split_axis=1, concat_axis=0, tiled=True)  27.8 us
    all_gather x1, waiting for transfers between devices, on_device(): keys = lax.all_gather(group_keys, 'tm', axis=0, tiled=True)  19.1 us
  transfers between devices with their start and end apart: 7, of which 6 were waited for; matrix products, arithmetic and copies ran while one was open for 16% of the time, Pallas kernels for 0%

commit v1 on v0

v1 whole, which is shorter than its diff:
```python
import functools
import math

import jax
import jax.numpy as jnp
from jax import lax
from jax.experimental import pallas as pl
from jax.experimental.pallas import tpu as pltpu
from jax.sharding import Mesh, PartitionSpec as P


HD = 128
HEADS = 32
BLOCK = 128
KEY_TILES = 32
GROUP = 8
Q_DEV = 16
NEG = -1e30
AXES = ("tm", "y", "zl", "x", "c")
PLANE = ("y", "x", "c")
NT = (((1,), (1,)), ((), ()))


def eye_mask():
    rows = lax.broadcasted_iota(jnp.int32, (BLOCK, BLOCK), 0)
    columns = lax.broadcasted_iota(jnp.int32, (BLOCK, BLOCK), 1)
    return rows == columns


def attention_kernel(place_ref, slot_ref, mask_ref, *refs):
    q_refs, kv_ref, o_ref = refs[:4], refs[4], refs[5]
    score_refs, high_refs, total_refs, sum_ref = refs[6:8], refs[8:10], refs[10:12], refs[12]
    scale = HD ** -0.5
    scale2 = scale * math.log2(math.e)
    plane = place_ref[0]

    def prepare(s):
        high_refs[s % 2][...] = jnp.full((4, BLOCK, BLOCK), NEG, jnp.float32)

    def score(s, t):
        source = lax.rem(plane - s + 4, 4)
        frame = slot_ref[lax.div(source, 2) * 8]
        q = q_refs[s][...]
        for pair in range(GROUP // 2):
            first = t * GROUP + pair * 2
            tiles = [kv_ref[first + u, :BLOCK] for u in range(2)]
            result = lax.dot_general(
                q, jnp.concatenate(tiles, 0), NT, preferred_element_type=jnp.float32
            )
            slot = lax.div(plane, 2) * 8 + lax.div(first, 8) * 2 + lax.rem(plane, 2)
            base = slot_ref[slot] * 8 + lax.rem(first, 8)
            for i in range(4):
                high = high_refs[s % 2][i]
                for u in range(2):
                    allowed = mask_ref[frame, 2 * i + lax.rem(source, 2), base + u] > 0
                    part = result[i * BLOCK : (i + 1) * BLOCK, u * BLOCK : (u + 1) * BLOCK]
                    part = jnp.where(allowed, part, NEG)
                    score_refs[s % 2][i, first + u] = part
                    high = jnp.maximum(high, part)
                high_refs[s % 2][i] = high

    def settle_high(s):
        for i in range(4):
            high = jnp.max(high_refs[s % 2][i], axis=1, keepdims=True)
            high_refs[s % 2][i] = jnp.broadcast_to(high, (BLOCK, BLOCK))
        total_refs[s % 2][...] = jnp.zeros((4, BLOCK, BLOCK), jnp.float32)
        sum_ref[...] = jnp.zeros((4 * BLOCK, HD), jnp.float32)

    def weigh(s, t):
        rows = []
        for i in range(4):
            high = high_refs[s % 2][i]
            total = total_refs[s % 2][i]
            parts = []
            for u in range(GROUP):
                w = jnp.exp2((score_refs[s % 2][i, t * GROUP + u] - high) * scale2)
                total = total + w
                parts.append(w.astype(jnp.bfloat16))
            total_refs[s % 2][i] = total
            rows.append(jnp.concatenate(parts, 1))
        values = jnp.concatenate([kv_ref[t * GROUP + u, BLOCK : 2 * BLOCK] for u in range(GROUP)], 0)
        sum_ref[...] += jnp.dot(jnp.concatenate(rows, 0), values, preferred_element_type=jnp.float32)

    def close(s):
        source = lax.rem(plane - s + 4, 4)
        pieces = []
        for i in range(4):
            denom = jnp.sum(total_refs[s % 2][i], axis=1, keepdims=True)
            high = jnp.max(high_refs[s % 2][i], axis=1, keepdims=True)
            done = (sum_ref[pl.ds(i * BLOCK, BLOCK), :] / denom).astype(jnp.bfloat16)
            for x in range(4):
                for core in range(2):
                    row = x * 32 + core * 16
                    o_ref[source * 2 + core, pl.ds(i * 64 + x * 16, 16), :] = done[row : row + 16]
            level = jnp.where(high > 0.5 * NEG, high * scale + jnp.log(denom), NEG)
            line = jnp.sum(jnp.where(eye_mask(), level, 0.0), axis=0, keepdims=True)
            first = line.astype(jnp.bfloat16)
            rest = line - first.astype(jnp.float32)
            second = rest.astype(jnp.bfloat16)
            third = (rest - second.astype(jnp.float32)).astype(jnp.bfloat16)
            pieces += [first, second, third]
        pieces.append(jnp.zeros((4, HD), jnp.bfloat16))
        for core in range(2):
            o_ref[source * 2 + core, pl.ds(256, 16), :] = jnp.concatenate(pieces, 0)

    def loop(body):
        def step(t, carry):
            body(t)
            return carry

        lax.fori_loop(0, KEY_TILES // GROUP, step, 0)

    prepare(0)
    loop(lambda t: score(0, t))
    for s in range(4):
        settle_high(s)
        if s < 3:
            prepare(s + 1)

        def step(t, s=s):
            weigh(s, t)
            if s < 3:
                score(s + 1, t)

        loop(step)
        close(s)


def attend(plane, slot_frame, radial_mask, queries, cache):
    vmem = pl.BlockSpec(memory_space=pltpu.VMEM)
    smem = pl.BlockSpec(memory_space=pltpu.SMEM)
    square = pltpu.VMEM((4, BLOCK, BLOCK), jnp.float32)
    scores = pltpu.VMEM((4, KEY_TILES, BLOCK, BLOCK), jnp.float32)
    return pl.pallas_call(
        attention_kernel,
        out_shape=jax.ShapeDtypeStruct((8, 272, HD), jnp.bfloat16),
        in_specs=[smem] * 3 + [vmem] * 5,
        out_specs=vmem,
        scratch_shapes=[scores] * 2 + [square] * 4 + [pltpu.VMEM((4 * BLOCK, HD), jnp.float32)],
        cost_estimate=pl.CostEstimate(
            flops=4 * 2048 * 4096 * HD, bytes_accessed=4 * 2**20, transcendentals=2048 * 4096
        ),
        name="attend",
    )(plane, slot_frame, radial_mask, *queries, cache)


def merge_kernel(core_ref, part_ref, out_ref):
    rows = lax.broadcasted_iota(jnp.int32, (64, BLOCK), 0)
    columns = lax.broadcasted_iota(jnp.int32, (64, BLOCK), 1)
    mine = columns == (rows // 16) * 32 + core_ref[0] * 16 + rows % 16
    for head in range(2):
        tails = [part_ref[2 * p + head, pl.ds(256, 16), :].astype(jnp.float32) for p in range(4)]
        for i in range(4):
            levels = [
                tail[3 * i : 3 * i + 1] + tail[3 * i + 1 : 3 * i + 2] + tail[3 * i + 2 : 3 * i + 3]
                for tail in tails
            ]
            high = functools.reduce(jnp.maximum, levels)
            shares = [jnp.exp(level - high) for level in levels]
            whole = functools.reduce(jnp.add, shares)
            summed = jnp.zeros((64, HD), jnp.float32)
            for p in range(4):
                column = jnp.sum(jnp.where(mine, shares[p] / whole, 0.0), axis=1, keepdims=True)
                part = part_ref[2 * p + head, pl.ds(i * 64, 64), :].astype(jnp.float32)
                summed = summed + part * column
            out_ref[pl.ds(i * 64, 64), head * HD : (head + 1) * HD] = summed.astype(jnp.bfloat16)


def merge(core, parts):
    vmem = pl.BlockSpec(memory_space=pltpu.VMEM)
    return pl.pallas_call(
        merge_kernel,
        out_shape=jax.ShapeDtypeStruct((256, 2 * HD), jnp.bfloat16),
        in_specs=[pl.BlockSpec(memory_space=pltpu.SMEM), vmem],
        out_specs=vmem,
        name="merge",
    )(core, parts)


def project_kernel(place_ref, *refs):
    rows, weights, outs, (w_ref, total_ref) = refs[:4], refs[4:6], refs[6:10], refs[10:]
    y, x, core = place_ref[0], place_ref[1], place_ref[2]
    size = weights[0].shape[0] // 8
    for side in range(2):
        for pair in range(8):
            block = pair * 2 + lax.rem(core + side, 2)
            target = pl.ds(pl.multiple_of(block * size, 16), size)
            w_ref[target, :] = weights[side][pl.ds(pair * size, size), :]
    total = None
    for s in range(4):
        source = lax.rem(y - s + 4, 4)
        w = w_ref[:, pl.ds(pl.multiple_of(source * 256, 256), 256)]
        term = lax.dot_general(rows[s][...], w, NT, preferred_element_type=jnp.float32)
        total = term if total is None else total + term
    total_ref[...] = total
    for s in range(4):
        target = lax.rem(x + s, 4)
        for i in range(4):
            start = pl.multiple_of(i * 64 + target * 16, 16)
            outs[s][pl.ds(i * 16, 16), :] = total_ref[pl.ds(start, 16), :].astype(outs[s].dtype)


def project(place, rows, weights):
    vmem = pl.BlockSpec(memory_space=pltpu.VMEM)
    kinds = [jnp.float32] + [jnp.bfloat16] * 3
    return pl.pallas_call(
        project_kernel,
        out_shape=tuple(jax.ShapeDtypeStruct((64, 1280), kind) for kind in kinds),
        in_specs=[pl.BlockSpec(memory_space=pltpu.SMEM)] + [vmem] * 6,
        out_specs=(vmem,) * 4,
        scratch_shapes=[
            pltpu.VMEM((1280, 8 * HD), jnp.bfloat16),
            pltpu.VMEM((256, 1280), jnp.float32),
        ],
        name="project",
    )(place, *rows, *weights)


def pack_query_kernel(place_ref, near_ref, far_ref, *out_refs):
    x, core = place_ref[1], place_ref[2]
    for s in range(4):
        for y in range(4):
            head = y * 8 + lax.rem(x + s, 4) * 2 + core
            columns = pl.ds(pl.multiple_of(head * HD, HD), HD)
            for side, w_ref in enumerate((near_ref, far_ref)):
                out_refs[s][side, :, y * HD : (y + 1) * HD] = w_ref[:, columns]


def pack_query(place, near, far):
    vmem = pl.BlockSpec(memory_space=pltpu.VMEM)
    rows = near.shape[0]
    return pl.pallas_call(
        pack_query_kernel,
        out_shape=(jax.ShapeDtypeStruct((2, rows, 4 * HD), jnp.bfloat16),) * 4,
        in_specs=[pl.BlockSpec(memory_space=pltpu.SMEM), vmem, vmem],
        out_specs=(vmem,) * 4,
        name="pack_query",
    )(place, near, far)


def pack_cache_kernel(k_ref, v_ref, out_ref):
    for head in range(HEADS):
        out_ref[head, :BLOCK, :] = k_ref[:, head * HD : (head + 1) * HD]
        out_ref[head, BLOCK:, :] = v_ref[:, head * HD : (head + 1) * HD]


def pack_cache(keys, values):
    vmem = pl.BlockSpec(memory_space=pltpu.VMEM)
    return pl.pallas_call(
        pack_cache_kernel,
        out_shape=jax.ShapeDtypeStruct((HEADS, 2 * BLOCK, HD), jnp.bfloat16),
        in_specs=[vmem, vmem],
        out_specs=vmem,
        name="pack_cache",
    )(keys, values)


def pack_tokens_kernel(token_ref, out_ref):
    width = out_ref.shape[2]
    for target in range(HEADS):
        column = target // 8 * width
        out_ref[target] = token_ref[:, column : column + width]


def pack_tokens(tokens):
    vmem = pl.BlockSpec(memory_space=pltpu.VMEM)
    return pl.pallas_call(
        pack_tokens_kernel,
        out_shape=jax.ShapeDtypeStruct((HEADS, Q_DEV, tokens.shape[1] // 4), jnp.bfloat16),
        in_specs=[vmem],
        out_specs=vmem,
        name="pack_tokens",
    )(tokens)


def settle_kernel(place_ref, *refs):
    parts, out_ref = refs[:4], refs[4]
    x = place_ref[1]
    size = parts[0].shape[1]
    for side in range(2):
        for s in range(4):
            block = side * 4 + lax.rem(x - s + 4, 4)
            out_ref[pl.ds(pl.multiple_of(block * size, 16), size), :] = parts[s][side]


def settle(place, parts):
    vmem = pl.BlockSpec(memory_space=pltpu.VMEM)
    _, rows, columns = parts[0].shape
    return pl.pallas_call(
        settle_kernel,
        out_shape=jax.ShapeDtypeStruct((8 * rows, columns), jnp.bfloat16),
        in_specs=[pl.BlockSpec(memory_space=pltpu.SMEM)] + [vmem] * 4,
        out_specs=vmem,
        name="settle",
    )(place, *parts)


def finish_kernel(place_ref, *refs):
    parts, out_ref = refs[:4], refs[4]
    width = parts[0].shape[1]
    for s in range(4):
        source = lax.rem(place_ref[0] - s + 4, 4)
        columns = pl.ds(pl.multiple_of(source * width, HD), width)
        out_ref[:, columns] = parts[s][...]


def finish(place, parts):
    vmem = pl.BlockSpec(memory_space=pltpu.VMEM)
    rows, width = parts[0].shape
    return pl.pallas_call(
        finish_kernel,
        out_shape=jax.ShapeDtypeStruct((rows, 4 * width), jnp.bfloat16),
        in_specs=[pl.BlockSpec(memory_space=pltpu.SMEM)] + [vmem] * 4,
        out_specs=vmem,
        name="finish",
    )(place, *parts)


def add_kernel(place_ref, *refs):
    parts, outs, total_ref = refs[:4], refs[4:8], refs[8]
    total = parts[0][...]
    for part in parts[1:]:
        total = total + part[...].astype(jnp.float32)
    total_ref[...] = total
    for s in range(4):
        start = pl.multiple_of(lax.rem(place_ref[0] + s, 4) * Q_DEV, Q_DEV)
        outs[s][...] = total_ref[pl.ds(start, Q_DEV), :].astype(jnp.bfloat16)


def add_parts(place, parts):
    vmem = pl.BlockSpec(memory_space=pltpu.VMEM)
    rows, width = parts[0].shape
    return pl.pallas_call(
        add_kernel,
        out_shape=(jax.ShapeDtypeStruct((Q_DEV, width), jnp.bfloat16),) * 4,
        in_specs=[pl.BlockSpec(memory_space=pltpu.SMEM)] + [vmem] * 4,
        out_specs=(vmem,) * 4,
        scratch_shapes=[pltpu.VMEM((rows, width), jnp.float32)],
        name="add_parts",
    )(place, *parts)


def pack_out_kernel(place_ref, *refs):
    x, zl = place_ref[1], place_ref[3]
    halves, out_refs = refs[:4], refs[4:]
    for s in range(4):
        for z_side in range(2):
            side = lax.rem(zl + z_side, 2)
            for y in range(4):
                head = y % 2 * 8 + lax.rem(x + s, 4) * 2
                columns = pl.ds(pl.multiple_of(head * HD, 2 * HD), 2 * HD)
                block = halves[z_side * 2 + y // 2][:, columns]
                out_refs[s][side, :, y * 2 * HD : (y + 1) * 2 * HD] = block


def pack_out(place, halves):
    vmem = pl.BlockSpec(memory_space=pltpu.VMEM)
    rows = halves[0].shape[0]
    return pl.pallas_call(
        pack_out_kernel,
        out_shape=(jax.ShapeDtypeStruct((2, rows, 8 * HD), jnp.bfloat16),) * 4,
        in_specs=[pl.BlockSpec(memory_space=pltpu.SMEM)] + [vmem] * 4,
        out_specs=(vmem,) * 4,
        name="pack_out",
    )(place, *halves)


def query_kernel(place_ref, token_ref, *refs):
    weights, out_refs, (w_ref, total_ref) = refs[:8], refs[8:12], refs[12:]
    y, x, core, zl = place_ref[0], place_ref[1], place_ref[2], place_ref[3]
    size = weights[0].shape[1]
    for z_side in range(2):
        for side in range(2):
            for s in range(4):
                block = lax.rem(zl + z_side, 2) * 8 + lax.rem(x - s + 4, 4) * 2
                block = block + lax.rem(core + side, 2)
                rows = pl.ds(pl.multiple_of(block * size, 16), size)
                w_ref[rows, :] = weights[z_side * 4 + s][side]
    total_ref[...] = jnp.dot(token_ref[...], w_ref[...], preferred_element_type=jnp.float32)
    for s in range(4):
        columns = pl.ds(pl.multiple_of(lax.rem(y + s, 4) * HD, HD), HD)
        out_refs[s][...] = total_ref[:, columns]


def query_parts(place, token_rows, weights):
    vmem = pl.BlockSpec(memory_space=pltpu.VMEM)
    rows, depth = token_rows.shape
    return pl.pallas_call(
        query_kernel,
        out_shape=(jax.ShapeDtypeStruct((rows, HD), jnp.float32),) * 4,
        in_specs=[pl.BlockSpec(memory_space=pltpu.SMEM)] + [vmem] * 9,
        out_specs=(vmem,) * 4,
        scratch_shapes=[
            pltpu.VMEM((depth, 4 * HD), jnp.bfloat16),
            pltpu.VMEM((rows, 4 * HD), jnp.float32),
        ],
        cost_estimate=pl.CostEstimate(
            flops=2 * rows * depth * 4 * HD, bytes_accessed=4 * 2**20, transcendentals=0
        ),
        name="query_parts",
    )(place, token_rows, *weights)


def z_shift(value, shift):
    return lax.ppermute(value, ("tm", "zl"), [(i, (i + shift) % 4) for i in range(4)])


def ring_shift(value, axis, shift):
    return lax.ppermute(value, axis, [(i, (i + shift) % 4) for i in range(4)])


def core_swap(value):
    return lax.ppermute(value, "c", [(0, 1), (1, 0)])


def exchange(table, axes):
    return lax.all_to_all(table, axes, split_axis=0, concat_axis=0, tiled=True)


def on_device(tokens, w_query, w_out, k_cache, v_cache, radial_mask, slot_frame):
    plane = (lax.axis_index("tm") * 2 + lax.axis_index("zl")).reshape(1)
    core = lax.axis_index("c").reshape(1)
    place = jnp.stack([lax.axis_index(a) for a in ("y", "x", "c", "zl")])

    packed = pack_query(place, w_query, core_swap(w_query))
    got = [packed[0]] + [ring_shift(packed[s], "x", s) for s in (1, 2, 3)]
    weights = got + [z_shift(got[s], 1) for s in (0, 1)] + [z_shift(got[s], -1) for s in (2, 3)]

    token_rows = exchange(pack_tokens(tokens), PLANE)

    half = w_out.shape[0] // 2
    low, high = w_out[:half].T, w_out[half:].T
    packed_out = pack_out(place, (low, high, z_shift(low, 1), z_shift(high, -1)))
    cache = pack_cache(k_cache, v_cache)
    ready = lax.optimization_barrier((weights, packed_out, cache, token_rows))
    weights, packed_out, cache, token_rows = ready

    partial = query_parts(place, token_rows.reshape(-1, token_rows.shape[2]), weights)
    partial, cache, packed_out = lax.optimization_barrier((partial, cache, packed_out))
    partial = [partial[0]] + [ring_shift(partial[s], "y", s) for s in (1, 2, 3)]
    arrived = exchange(cache, PLANE)
    got = [packed_out[0]] + [ring_shift(packed_out[s], "x", s) for s in (1, 2, 3)]

    query = functools.reduce(jnp.add, partial).astype(jnp.bfloat16)
    queries = [query] + [z_shift(query, s) for s in (1, 2, 3)]
    outs = attend(plane, slot_frame, radial_mask, queries, arrived)

    got, outs = lax.optimization_barrier((got, outs))
    out_near = settle(place, got)
    out_far = core_swap(out_near)
    parts = exchange(outs, ("tm", "zl", "c"))
    attended = merge(core, parts)
    rows = [attended] + [ring_shift(attended, "y", s) for s in (1, 2, 3)]
    parts = project(place, rows, (out_near, out_far))
    parts = [parts[0]] + [ring_shift(parts[s], "x", s) for s in (1, 2, 3)]
    parts = add_parts(place, parts)
    parts = [parts[0]] + [ring_shift(parts[s], "y", s) for s in (1, 2, 3)]
    return finish(place, parts)


def solution(mesh):
    fine = Mesh(mesh.devices.reshape(2, 4, 2, 4, 2), AXES)
    return jax.shard_map(
        on_device,
        mesh=fine,
        in_specs=(
            P(AXES, None),
            P(("y", "zl", "x", "c"), None),
            P(None, ("y", "zl", "x", "c")),
            P(AXES, None),
            P(AXES, None),
            P(),
            P(),
        ),
        out_specs=P(AXES, None),
        check_vma=False,
    )
```

time: 715 us -> 186 us (0.26)
  waiting for transfers between devices: 506 us -> 58.5 us
  matrix products: 82.5 us -> 0 us
  Pallas kernels: 0 us -> 43 us
  starting transfers between devices: 28.4 us -> 59.2 us
  other arithmetic: 28.5 us -> 0.73 us
  blocking collectives: 33.8 us -> 15.2 us
  between operations: 15.4 us -> 0.29 us
  local copies, waits for them, and re-layouts: 16.1 us -> 7.83 us
    reduce_scatter x1 -> x0, waiting for transfers between devices: 321 us -> none  [on_device(): lax.psum_scatter((partial_value * part_pick).reshape(lax.axis_size('seq')...]
    all_to_all x4 -> x2, waiting for transfers between devices: 103 us -> 0.01 us  [exchange(): return lax.all_to_all(table, axes, split_axis=0, concat_axis=0, tiled=True)]
    dot_general x68 -> x0, matrix products: 82.5 us -> none  [the longest x32 38.6 us: one_tile(): jnp.einsum('qhd,khd->qhk', query, k_tile, preferred_element_type=jnp.floa...]
    all_gather x2 -> x0, waiting for transfers between devices: 80.1 us -> none  [the longest x1 61 us: on_device(): values = lax.all_gather(group_values, 'tm', axis=0, tiled=True)]
    ppermute x0 -> x29, waiting for transfers between devices: none -> 58.5 us  [the longest x18 57.7 us: ring_shift(): return lax.ppermute(value, axis, [(i, (i + shift) % 4) for i in range(4)])]
    ppermute x0 -> x29, starting transfers between devices: none -> 46.8 us  [the longest x18 31.5 us: ring_shift(): return lax.ppermute(value, axis, [(i, (i + shift) % 4) for i in range(4)])]
    pallas_call x0 -> x11, Pallas kernels: none -> 43 us  [the longest x1 16.8 us: attend(): pl.pallas_call(attention_kernel, out_shape=jax.ShapeDtypeStruct((8, 272,...]
    all_to_all x1, blocking collectives: 33.8 us -> 15.2 us  [exchange(): return lax.all_to_all(table, axes, split_axis=0, concat_axis=0, tiled=True)]
  transfers between devices with their start and end apart: 7 -> 31, of which waited for: 6 -> 14; matrix products, arithmetic and copies ran while one was open for 16% -> 0% of each run, Pallas kernels for 0% -> 15%
where the time goes in v1:
time: 186 us; the launch traced here: 185 us
  starting transfers between devices  59.2 us (32%)
  waiting for transfers between devices  58.5 us (31%)
  Pallas kernels  43 us (23%)
  blocking collectives  15.2 us (8%)
  local copies, waits for them, and re-layouts  7.83 us (4%)
    ppermute x18, waiting for transfers between devices, ring_shift(): return lax.ppermute(value, axis, [(i, (i + shift) % 4) for i in range(4)])  57.7 us
    ppermute x18, starting transfers between devices, ring_shift(): return lax.ppermute(value, axis, [(i, (i + shift) % 4) for i in range(4)])  31.5 us
    pallas_call x1, Pallas kernels, attend(): pl.pallas_call(attention_kernel, out_shape=jax.ShapeDtypeStruct((8, 272,...  16.8 us
    all_to_all x1, blocking collectives, exchange(): return lax.all_to_all(table, axes, split_axis=0, concat_axis=0, tiled=True)  15.2 us
    ppermute x9, starting transfers between devices, z_shift(): lax.ppermute(value, ('tm', 'zl'), [(i, (i + shift) % 4) for i in range(4)])  15 us
    all_to_all x2, starting transfers between devices, exchange(): return lax.all_to_all(table, axes, split_axis=0, concat_axis=0, tiled=True)  12.4 us
    unnamed x66, local copies, waits for them, and re-layouts  7.78 us
    pallas_call x1, Pallas kernels, project(): pl.pallas_call(project_kernel, out_shape=tuple((jax.ShapeDtypeStruct((64,...  4.16 us
  transfers between devices with their start and end apart: 31, of which 14 were waited for; matrix products, arithmetic and copies ran while one was open for 0% of the time, Pallas kernels for 15%

profile of v1, /device:TPU:0, one launch (start us, length us, event | category | flops | bytes accessed | tf_op | source)
XLA Modules:
  0.0 184.7 jit_solution(159357902036040357)
XLA Ops:
  0.0 2.1 %pack_tokens.1 = bf16[32,16,1280]{2,1,0:T(8,128)(2,1)} custom-call(bf16[16,5120]{1,0:T(8,128)(2,1)} %token_ref.1), custom_call_target="tpu_custom_call" | custom-call | tf_op jit(solution)/shard_map/pack_tokens/pallas_call | solution.py:267
  2.1 7.6 %all-to-all-start = ((bf16[32,16,1280]{2,1,0:T(8,128)(2,1)}), bf16[32,16,1280]{2,1,0:T(8,128)(2,1)S(1)}, u32[]{:S(2)}, u32[]{:S(2)}) async-start(bf16[32,16,1280]{2,1,0:T(8,128)(2,1)} %pack_tokens.1), calls=%async_computation | async-start | bytes 2621440 | tf_op jit(solution)/shard_map/all_to_all | solution.py:417
  10.1 4.1 %collective-permute-start.9 = (bf16[80,2048]{1,0:T(8,128)(2,1)S(1)}, bf16[80,2048]{1,0:T(8,128)(2,1)S(1)}, u32[]{:S(2)}, u32[]{:S(2)}) collective-permute-start(bf16[80,2048]{1,0:T(8,128)(2,1)S(1)} %get-tuple-element.101.refs_1_), channel_id=1, source_target_pairs={{0,72},{8,0},{64,8},{72,64},{1,73},{9,1},{65,9},{73,65},{2,74},{10... | collective-permute-start | bytes 983048 | tf_op jit(solution)/shard_map/ppermute | solution.py:405
  14.9 2.3 %pack_query.1 = (bf16[2,80,512]{2,1,0:T(8,128)(2,1)}, bf16[2,80,512]{2,1,0:T(8,128)(2,1)}, bf16[2,80,512]{2,1,0:T(8,128)(2,1)}, bf16[2,80,512]{2,1,0:T(8,128)(2,1)}) custom-call(s32[4]{0:T(128)} %pad_add_fusion.place_ref, bf16[80,4096]{1,0:T(8,128)(2,1)} %near_ref.1, bf16[80,4096]{1,0:T(8,128)(2,1)} %collective-permute-done.far_ref), custom_call_target="tpu_custom_call" | custom-call | tf_op jit(solution)/shard_map/pack_query/pallas_call | solution.py:232
  17.2 1.6 collective-permute-start.1
  18.8 2.7 %collective-permute-start.2 = (bf16[2,80,512]{2,1,0:T(8,128)(2,1)}, bf16[2,80,512]{2,1,0:T(8,128)(2,1)S(1)}, u32[]{:S(2)}, u32[]{:S(2)}) collective-permute-start(bf16[2,80,512]{2,1,0:T(8,128)(2,1)} %get-tuple-element.55), channel_id=1, source_target_pairs={{0,4},{2,6},{4,0},{6,2},{1,5},{3,7},{5,1},{7,3},{8,12},{10,14},{12... | collective-permute-start | bytes 491528 | tf_op jit(solution)/shard_map/ppermute | solution.py:409
  21.5 1.5 collective-permute-start.3
  22.9 8.3 %collective-permute-done.1.refs_1_ = bf16[2,80,512]{2,1,0:T(8,128)(2,1)S(1)} collective-permute-done((bf16[2,80,512]{2,1,0:T(8,128)(2,1)}, bf16[2,80,512]{2,1,0:T(8,128)(2,1)S(1)}, u32[]{:S(2)}, u32[]{:S(2)}) %collective-permute-start.1) | collective-permute-done | bytes 163872 | tf_op jit(solution)/shard_map/ppermute | solution.py:409
  31.3 1.9 %collective-permute-start.5 = (bf16[2,80,512]{2,1,0:T(8,128)(2,1)S(1)}, bf16[2,80,512]{2,1,0:T(8,128)(2,1)S(1)}, u32[]{:S(2)}, u32[]{:S(2)}) collective-permute-start(bf16[2,80,512]{2,1,0:T(8,128)(2,1)S(1)} %collective-permute-done.1.refs_1_), channel_id=1, source_target_pairs={{0,8},{8,64},{64,72},{72,0},{1,9},{9,65},{65,73},{73,1},{2,10},{10... | collective-permute-start | bytes 491528 | tf_op jit(solution)/shard_map/ppermute | solution.py:405
  33.2 2.1 %collective-permute-done.2.refs_2_ = bf16[2,80,512]{2,1,0:T(8,128)(2,1)S(1)} collective-permute-done((bf16[2,80,512]{2,1,0:T(8,128)(2,1)}, bf16[2,80,512]{2,1,0:T(8,128)(2,1)S(1)}, u32[]{:S(2)}, u32[]{:S(2)}) %collective-permute-start.2) | collective-permute-done | bytes 163872 | tf_op jit(solution)/shard_map/ppermute | solution.py:409
  35.3 4.0 %collective-permute-start.6 = (bf16[2,80,512]{2,1,0:T(8,128)(2,1)S(1)}, bf16[2,80,512]{2,1,0:T(8,128)(2,1)}, u32[]{:S(2)}, u32[]{:S(2)}) collective-permute-start(bf16[2,80,512]{2,1,0:T(8,128)(2,1)S(1)} %collective-permute-done.2.refs_2_), channel_id=1, source_target_pairs={{0,72},{8,0},{64,8},{72,64},{1,73},{9,1},{65,9},{73,65},{2,74},{10... | collective-permute-start | bytes 491528 | tf_op jit(solution)/shard_map/ppermute | solution.py:405
  39.8 3.2 %pack_cache.1 = bf16[32,256,128]{2,1,0:T(8,128)(2,1)} custom-call(bf16[128,4096]{1,0:T(8,128)(2,1)} %k_ref.1, bf16[128,4096]{1,0:T(8,128)(2,1)} %v_ref.1), custom_call_target="tpu_custom_call" | custom-call | tf_op jit(solution)/shard_map/pack_cache/pallas_call | solution.py:249
  43.0 0.7 copy-done.9
  43.8 2.5 %pack_out.1 = (bf16[2,80,1024]{2,1,0:T(8,128)(2,1)}, bf16[2,80,1024]{2,1,0:T(8,128)(2,1)}, bf16[2,80,1024]{2,1,0:T(8,128)(2,1)}, bf16[2,80,1024]{2,1,0:T(8,128)(2,1)}) custom-call(s32[4]{0:T(128)} %pad_add_fusion.place_ref, bf16[80,2048]{1,0:T(8,128)(2,1)} %copy-done.4, bf16[80,2048]{1,0:T(8,128)(2,1)} %copy-done.3, bf16[80,2048]{1,0:T(8,128)(2,1)} %copy-done.9, ...), custom_call_target="tpu_custom_call" | custom-call | tf_op jit(solution)/shard_map/pack_out/pallas_call | solution.py:359
  47.4 3.9 %query_parts.1 = (f32[512,128]{1,0:T(8,128)}, f32[512,128]{1,0:T(8,128)}, f32[512,128]{1,0:T(8,128)}, f32[512,128]{1,0:T(8,128)}) custom-call(s32[4]{0:T(128)} %pad_add_fusion.place_ref, bf16[512,1280]{1,0:T(8,128)(2,1)} %bitcast.10, bf16[2,80,512]{2,1,0:T(8,128)(2,1)} %get-tuple-element.62.refs_0_, bf16[2,80,512]{2,1,0:T(8,128)(2,1)} %copy-done.14, ...), custom_call_target="tpu_custom_call" | custom-call | flops 671088640 | bytes 4194304 | tf_op jit(solution)/shard_map/query_parts/pallas_call | solution.py:388
  51.3 4.9 %all-to-all-start.1 = ((bf16[32,256,128]{2,1,0:T(8,128)(2,1)}), bf16[32,256,128]{2,1,0:T(8,128)(2,1)S(1)}, u32[]{:S(2)}, u32[]{:S(2)}) async-start(bf16[32,256,128]{2,1,0:T(8,128)(2,1)} %pack_cache.1), calls=%async_computation.1 | async-start | bytes 4194304 | tf_op jit(solution)/shard_map/all_to_all | solution.py:417
  56.2 1.9 %collective-permute-start.13 = (f32[512,128]{1,0:T(8,128)S(1)}, f32[512,128]{1,0:T(8,128)S(1)}, u32[]{:S(2)}, u32[]{:S(2)}) collective-permute-start(f32[512,128]{1,0:T(8,128)S(1)} %copy-done.32), channel_id=1, source_target_pairs={{0,16},{16,32},{32,48},{48,0},{1,17},{17,33},{33,49},{49,1},{2,18}... | collective-permute-start | bytes 786440 | tf_op jit(solution)/shard_map/ppermute | solution.py:409
  58.1 2.7 %collective-permute-start.14 = (f32[512,128]{1,0:T(8,128)S(1)}, f32[512,128]{1,0:T(8,128)S(1)}, u32[]{:S(2)}, u32[]{:S(2)}) collective-permute-start(f32[512,128]{1,0:T(8,128)S(1)} %copy-done.31), channel_id=1, source_target_pairs={{0,32},{16,48},{32,0},{48,16},{1,33},{17,49},{33,1},{49,17},{2,34}... | collective-permute-start | bytes 786440 | tf_op jit(solution)/shard_map/ppermute | solution.py:409
  60.8 1.4 collective-permute-start.15
  62.2 26.5 %collective-permute-done.13 = f32[512,128]{1,0:T(8,128)S(1)} collective-permute-done((f32[512,128]{1,0:T(8,128)S(1)}, f32[512,128]{1,0:T(8,128)S(1)}, u32[]{:S(2)}, u32[]{:S(2)}) %collective-permute-start.13) | collective-permute-done | bytes 262176 | tf_op jit(solution)/shard_map/ppermute | solution.py:409
  88.7 5.6 %collective-permute-done.14 = f32[512,128]{1,0:T(8,128)S(1)} collective-permute-done((f32[512,128]{1,0:T(8,128)S(1)}, f32[512,128]{1,0:T(8,128)S(1)}, u32[]{:S(2)}, u32[]{:S(2)}) %collective-permute-start.14) | collective-permute-done | bytes 262176 | tf_op jit(solution)/shard_map/ppermute | solution.py:409
  94.4 3.5 %collective-permute-start.18 = (bf16[512,128]{1,0:T(8,128)(2,1)S(1)}, bf16[512,128]{1,0:T(8,128)(2,1)}, u32[]{:S(2)}, u32[]{:S(2)}) collective-permute-start(bf16[512,128]{1,0:T(8,128)(2,1)S(1)} %add_convert_fusion.refs_0_), channel_id=1, source_target_pairs={{0,72},{8,0},{64,8},{72,64},{1,73},{9,1},{65,9},{73,65},{2,74},{10... | collective-permute-start | bytes 393224 | tf_op jit(solution)/shard_map/ppermute | solution.py:405
  98.2 0.7 collective-permute-start.16
  98.9 1.5 collective-permute-start.10
  100.4 2.7 %collective-permute-start.11 = (bf16[2,80,1024]{2,1,0:T(8,128)(2,1)}, bf16[2,80,1024]{2,1,0:T(8,128)(2,1)S(1)}, u32[]{:S(2)}, u32[]{:S(2)}) collective-permute-start(bf16[2,80,1024]{2,1,0:T(8,128)(2,1)} %get-tuple-element.81), channel_id=1, source_target_pairs={{0,4},{2,6},{4,0},{6,2},{1,5},{3,7},{5,1},{7,3},{8,12},{10,14},{12... | collective-permute-start | bytes 983048 | tf_op jit(solution)/shard_map/ppermute | solution.py:409
  103.2 2.9 %collective-permute-start.12 = (bf16[2,80,1024]{2,1,0:T(8,128)(2,1)S(1)}, bf16[2,80,1024]{2,1,0:T(8,128)(2,1)S(1)}, u32[]{:S(2)}, u32[]{:S(2)}) collective-permute-start(bf16[2,80,1024]{2,1,0:T(8,128)(2,1)S(1)} %copy-done.29), channel_id=1, source_target_pairs={{0,6},{2,0},{4,2},{6,4},{1,7},{3,1},{5,3},{7,5},{8,14},{10,8},{12,... | collective-permute-start | bytes 983048 | tf_op jit(solution)/shard_map/ppermute | solution.py:409
  106.8 1.4 copy-done.1
  108.1 16.8 %attend.1 = bf16[8,272,128]{2,1,0:T(8,128)(2,1)} custom-call(s32[1]{0:T(128)} %bitcast.7.place_ref, s32[16]{0:T(128)} %slot_ref.1, s32[16,8,128]{2,1,0:T(8,128)} %mask_ref.1, bf16[512,128]{1,0:T(8,128)(2,1)} %copy-done.22, bf16[512,128]{1,0:T(8,128)(2,1)} %collective-permute-done.16.refs_1_, bf16[512,128]{1,0:T(8,128)(2,1)} %collective-permute-done.17.refs_2_, ...), custom_call_target="tpu_custom_call" | custom-call | flops 4294967296 | bytes 4194304 | tf_op jit(solution)/shard_map/attend/pallas_call | solution.py:134
  125.8 0.7 copy-done.12
  126.5 2.4 %settle.1.refs_4_ = bf16[640,1024]{1,0:T(8,128)(2,1)} custom-call(s32[4]{0:T(128)} %pad_add_fusion.place_ref, bf16[2,80,1024]{2,1,0:T(8,128)(2,1)} %get-tuple-element.89.refs_0_, bf16[2,80,1024]{2,1,0:T(8,128)(2,1)} %copy-done.10, bf16[2,80,1024]{2,1,0:T(8,128)(2,1)} %copy-done.11, bf16[2,80,1024]{2,1,0:T(8,128)(2,1)} %copy-done.12), custom_call_target="tpu_custom_call" | custom-call | tf_op jit(solution)/shard_map/settle/pallas_call | solution.py:289
  128.9 15.2 %all_to_all.15.part_ref = bf16[8,272,128]{2,1,0:T(8,128)(2,1)} all-to-all(bf16[8,272,128]{2,1,0:T(8,128)(2,1)S(1)} %copy-done.7), channel_id=1, replica_groups=mesh['tm'=2,'y'=4,'zl'=2,'x'=4,'c'=2] {'tm','zl','c'}, dimensions={0} | all-to-all | bytes 1114112 | tf_op jit(solution)/shard_map/all_to_all | solution.py:417
  144.1 2.1 %merge.1.refs_0_ = bf16[256,256]{1,0:T(8,128)(2,1)} custom-call(s32[1]{0:T(128)} %bitcast.2.core_ref, bf16[8,272,128]{2,1,0:T(8,128)(2,1)} %all_to_all.15.part_ref), custom_call_target="tpu_custom_call" | custom-call | tf_op jit(solution)/shard_map/merge/pallas_call | solution.py:171
  146.4 2.1 %collective-permute-start.20 = (bf16[256,256]{1,0:T(8,128)(2,1)}, bf16[256,256]{1,0:T(8,128)(2,1)S(1)}, u32[]{:S(2)}, u32[]{:S(2)}) collective-permute-start(bf16[256,256]{1,0:T(8,128)(2,1)} %merge.1.refs_0_), channel_id=1, source_target_pairs={{0,32},{16,48},{32,0},{48,16},{1,33},{17,49},{33,1},{49,17},{2,34}... | collective-permute-start | bytes 393224 | tf_op jit(solution)/shard_map/ppermute | solution.py:409
  148.5 1.1 collective-permute-start.19
  149.6 3.2 %collective-permute-done.21.refs_3_ = bf16[256,256]{1,0:T(8,128)(2,1)S(1)} collective-permute-done((bf16[256,256]{1,0:T(8,128)(2,1)}, bf16[256,256]{1,0:T(8,128)(2,1)S(1)}, u32[]{:S(2)}, u32[]{:S(2)}) %collective-permute-start.21) | collective-permute-done | bytes 131104 | tf_op jit(solution)/shard_map/ppermute | solution.py:409
  152.8 1.2 collective-permute-done.20.refs_2_
  154.0 2.1 %collective-permute-done.19.refs_1_ = bf16[256,256]{1,0:T(8,128)(2,1)S(1)} collective-permute-done((bf16[256,256]{1,0:T(8,128)(2,1)}, bf16[256,256]{1,0:T(8,128)(2,1)S(1)}, u32[]{:S(2)}, u32[]{:S(2)}) %collective-permute-start.19) | collective-permute-done | bytes 131104 | tf_op jit(solution)/shard_map/ppermute | solution.py:409
  156.7 1.1 copy-done.2
  157.8 4.2 %project.1 = (f32[64,1280]{1,0:T(8,128)}, bf16[64,1280]{1,0:T(8,128)(2,1)}, bf16[64,1280]{1,0:T(8,128)(2,1)}, bf16[64,1280]{1,0:T(8,128)(2,1)}) custom-call(s32[4]{0:T(128)} %pad_add_fusion.place_ref, bf16[256,256]{1,0:T(8,128)(2,1)} %merge.1.refs_0_, bf16[256,256]{1,0:T(8,128)(2,1)} %copy-done.25, bf16[256,256]{1,0:T(8,128)(2,1)} %copy-done.24, ...), custom_call_target="tpu_custom_call" | custom-call | tf_op jit(solution)/shard_map/project/pallas_call | solution.py:206
  162.4 2.6 %collective-permute-start.24 = (bf16[64,1280]{1,0:T(8,128)(2,1)}, bf16[64,1280]{1,0:T(8,128)(2,1)S(1)}, u32[]{:S(2)}, u32[]{:S(2)}) collective-permute-start(bf16[64,1280]{1,0:T(8,128)(2,1)} %get-tuple-element.95), channel_id=1, source_target_pairs={{0,4},{2,6},{4,0},{6,2},{1,5},{3,7},{5,1},{7,3},{8,12},{10,14},{12... | collective-permute-start | bytes 491528 | tf_op jit(solution)/shard_map/ppermute | solution.py:409
  165.0 1.7 collective-permute-start.25
  166.7 6.0 %collective-permute-done.23.refs_1_ = bf16[64,1280]{1,0:T(8,128)(2,1)S(1)} collective-permute-done((bf16[64,1280]{1,0:T(8,128)(2,1)}, bf16[64,1280]{1,0:T(8,128)(2,1)S(1)}, u32[]{:S(2)}, u32[]{:S(2)}) %collective-permute-start.23) | collective-permute-done | bytes 163872 | tf_op jit(solution)/shard_map/ppermute | solution.py:409
  173.9 2.0 %add_parts.1 = (bf16[16,1280]{1,0:T(8,128)(2,1)}, bf16[16,1280]{1,0:T(8,128)(2,1)}, bf16[16,1280]{1,0:T(8,128)(2,1)}, bf16[16,1280]{1,0:T(8,128)(2,1)}) custom-call(s32[4]{0:T(128)} %pad_add_fusion.place_ref, f32[64,1280]{1,0:T(8,128)} %get-tuple-element.93.refs_0_, bf16[64,1280]{1,0:T(8,128)(2,1)} %copy-done.19, bf16[64,1280]{1,0:T(8,128)(2,1)} %copy-done.20, ...), custom_call_target="tpu_custom_call" | custom-call | tf_op jit(solution)/shard_map/add_parts/pallas_call | solution.py:333
  175.9 2.1 %collective-permute-start.27 = (bf16[16,1280]{1,0:T(8,128)(2,1)}, bf16[16,1280]{1,0:T(8,128)(2,1)S(1)}, u32[]{:S(2)}, u32[]{:S(2)}) collective-permute-start(bf16[16,1280]{1,0:T(8,128)(2,1)} %get-tuple-element.99), channel_id=1, source_target_pairs={{0,32},{16,48},{32,0},{48,16},{1,33},{17,49},{33,1},{49,17},{2,34}... | collective-permute-start | bytes 122888 | tf_op jit(solution)/shard_map/ppermute | solution.py:409
  178.0 2.4 %collective-permute-start.28 = (bf16[16,1280]{1,0:T(8,128)(2,1)}, bf16[16,1280]{1,0:T(8,128)(2,1)S(1)}, u32[]{:S(2)}, u32[]{:S(2)}) collective-permute-start(bf16[16,1280]{1,0:T(8,128)(2,1)} %get-tuple-element.100), channel_id=1, source_target_pairs={{0,48},{16,0},{32,16},{48,32},{1,49},{17,1},{33,17},{49,33},{2,50}... | collective-permute-start | bytes 122888 | tf_op jit(solution)/shard_map/ppermute | solution.py:409
  180.4 0.9 collective-permute-done.26.refs_1_
  181.7 0.9 collective-permute-done.28.refs_3_
  183.2 1.5 finish.1
  (95 shorter events, 8.1 us)
Async XLA Ops:
  2.1 7.6 %copy-start.6 = (bf16[80,4096]{1,0:T(8,128)(2,1)S(1)}, bf16[80,4096]{1,0:T(8,128)(2,1)}, u32[]{:S(2)}) copy-start(bf16[80,4096]{1,0:T(8,128)(2,1)} %near_ref.1) | copy-start | bytes 1966084
  2.1 7.9 %copy-start.5 = (bf16[4096,80]{0,1:T(8,128)(2,1)S(1)}, bf16[4096,80]{0,1:T(8,128)(2,1)}, u32[]{:S(2)}) copy-start(bf16[4096,80]{0,1:T(8,128)(2,1)} %param.9) | copy-start | bytes 1966084
  2.1 44.3 %all-to-all-start = ((bf16[32,16,1280]{2,1,0:T(8,128)(2,1)}), bf16[32,16,1280]{2,1,0:T(8,128)(2,1)S(1)}, u32[]{:S(2)}, u32[]{:S(2)}) async-start(bf16[32,16,1280]{2,1,0:T(8,128)(2,1)} %pack_tokens.1), calls=%async_computation | async-start | bytes 2621440 | tf_op jit(solution)/shard_map/all_to_all | solution.py:417
  9.7 5.2 %collective-permute-start = (bf16[80,4096]{1,0:T(8,128)(2,1)S(1)}, bf16[80,4096]{1,0:T(8,128)(2,1)}, u32[]{:S(2)}, u32[]{:S(2)}) collective-permute-start(bf16[80,4096]{1,0:T(8,128)(2,1)S(1)} %copy-done.6), channel_id=1, source_target_pairs={{0,1},{1,0},{2,3},{3,2},{4,5},{5,4},{6,7},{7,6},{8,9},{9,8},{10,11... | collective-permute-start | bytes 1966088 | tf_op jit(solution)/shard_map/ppermute | solution.py:413
  10.1 32.9 %copy-start.3 = (bf16[80,2048]{1,0:T(8,128)(2,1)}, bf16[80,2048]{1,0:T(8,128)(2,1)S(1)}, u32[]{:S(2)}) copy-start(bf16[80,2048]{1,0:T(8,128)(2,1)S(1)} %get-tuple-element.101.refs_1_) | copy-start | bytes 983044
  10.1 32.9 %copy-start.4 = (bf16[80,2048]{1,0:T(8,128)(2,1)}, bf16[80,2048]{1,0:T(8,128)(2,1)S(1)}, u32[]{:S(2)}) copy-start(bf16[80,2048]{1,0:T(8,128)(2,1)S(1)} %get-tuple-element.102.refs_0_) | copy-start | bytes 983044
  10.1 12.8 %collective-permute-start.9 = (bf16[80,2048]{1,0:T(8,128)(2,1)S(1)}, bf16[80,2048]{1,0:T(8,128)(2,1)S(1)}, u32[]{:S(2)}, u32[]{:S(2)}) collective-permute-start(bf16[80,2048]{1,0:T(8,128)(2,1)S(1)} %get-tuple-element.101.refs_1_), channel_id=1, source_target_pairs={{0,72},{8,0},{64,8},{72,64},{1,73},{9,1},{65,9},{73,65},{2,74},{10... | collective-permute-start | bytes 983048 | tf_op jit(solution)/shard_map/ppermute | solution.py:405
  14.2 28.8 %collective-permute-start.8 = (bf16[80,2048]{1,0:T(8,128)(2,1)S(1)}, bf16[80,2048]{1,0:T(8,128)(2,1)S(1)}, u32[]{:S(2)}, u32[]{:S(2)}) collective-permute-start(bf16[80,2048]{1,0:T(8,128)(2,1)S(1)} %get-tuple-element.102.refs_0_), channel_id=1, source_target_pairs={{0,8},{8,64},{64,72},{72,0},{1,9},{9,65},{65,73},{73,1},{2,10},{10... | collective-permute-start | bytes 983048 | tf_op jit(solution)/shard_map/ppermute | solution.py:405
  17.2 14.1 %collective-permute-start.1 = (bf16[2,80,512]{2,1,0:T(8,128)(2,1)}, bf16[2,80,512]{2,1,0:T(8,128)(2,1)S(1)}, u32[]{:S(2)}, u32[]{:S(2)}) collective-permute-start(bf16[2,80,512]{2,1,0:T(8,128)(2,1)} %get-tuple-element.54), channel_id=1, source_target_pairs={{0,2},{2,4},{4,6},{6,0},{1,3},{3,5},{5,7},{7,1},{8,10},{10,12},{12... | collective-permute-start | bytes 491528 | tf_op jit(solution)/shard_map/ppermute | solution.py:409
  18.8 16.5 %collective-permute-start.2 = (bf16[2,80,512]{2,1,0:T(8,128)(2,1)}, bf16[2,80,512]{2,1,0:T(8,128)(2,1)S(1)}, u32[]{:S(2)}, u32[]{:S(2)}) collective-permute-start(bf16[2,80,512]{2,1,0:T(8,128)(2,1)} %get-tuple-element.55), channel_id=1, source_target_pairs={{0,4},{2,6},{4,0},{6,2},{1,5},{3,7},{5,1},{7,3},{8,12},{10,14},{12... | collective-permute-start | bytes 491528 | tf_op jit(solution)/shard_map/ppermute | solution.py:409
  21.5 17.9 %collective-permute-start.3 = (bf16[2,80,512]{2,1,0:T(8,128)(2,1)}, bf16[2,80,512]{2,1,0:T(8,128)(2,1)S(1)}, u32[]{:S(2)}, u32[]{:S(2)}) collective-permute-start(bf16[2,80,512]{2,1,0:T(8,128)(2,1)} %get-tuple-element.56), channel_id=1, source_target_pairs={{0,6},{2,0},{4,2},{6,4},{1,7},{3,1},{5,3},{7,5},{8,14},{10,8},{12,... | collective-permute-start | bytes 491528 | tf_op jit(solution)/shard_map/ppermute | solution.py:409
  22.9 20.1 %copy-start.8 = (bf16[80,2048]{1,0:T(8,128)(2,1)}, bf16[80,2048]{1,0:T(8,128)(2,1)S(1)}, u32[]{:S(2)}) copy-start(bf16[80,2048]{1,0:T(8,128)(2,1)S(1)} %collective-permute-done.9.refs_3_) | copy-start | bytes 983044
  22.9 23.3 %collective-permute-start.4 = (bf16[2,80,512]{2,1,0:T(8,128)(2,1)}, bf16[2,80,512]{2,1,0:T(8,128)(2,1)S(1)}, u32[]{:S(2)}, u32[]{:S(2)}) collective-permute-start(bf16[2,80,512]{2,1,0:T(8,128)(2,1)} %get-tuple-element.62.refs_0_), channel_id=1, source_target_pairs={{0,8},{8,64},{64,72},{72,0},{1,9},{9,65},{65,73},{73,1},{2,10},{10... | collective-permute-start | bytes 491528 | tf_op jit(solution)/shard_map/ppermute | solution.py:405
  31.3 11.7 %copy-start.14 = (bf16[2,80,512]{2,1,0:T(8,128)(2,1)}, bf16[2,80,512]{2,1,0:T(8,128)(2,1)S(1)}, u32[]{:S(2)}) copy-start(bf16[2,80,512]{2,1,0:T(8,128)(2,1)S(1)} %collective-permute-done.1.refs_1_) | copy-start | bytes 491524
  31.3 15.0 %collective-permute-start.5 = (bf16[2,80,512]{2,1,0:T(8,128)(2,1)S(1)}, bf16[2,80,512]{2,1,0:T(8,128)(2,1)S(1)}, u32[]{:S(2)}, u32[]{:S(2)}) collective-permute-start(bf16[2,80,512]{2,1,0:T(8,128)(2,1)S(1)} %collective-permute-done.1.refs_1_), channel_id=1, source_target_pairs={{0,8},{8,64},{64,72},{72,0},{1,9},{9,65},{65,73},{73,1},{2,10},{10... | collective-permute-start | bytes 491528 | tf_op jit(solution)/shard_map/ppermute | solution.py:405
  35.3 7.7 %copy-start.15 = (bf16[2,80,512]{2,1,0:T(8,128)(2,1)}, bf16[2,80,512]{2,1,0:T(8,128)(2,1)S(1)}, u32[]{:S(2)}) copy-start(bf16[2,80,512]{2,1,0:T(8,128)(2,1)S(1)} %collective-permute-done.2.refs_2_) | copy-start | bytes 491524
  35.3 11.0 %collective-permute-start.6 = (bf16[2,80,512]{2,1,0:T(8,128)(2,1)S(1)}, bf16[2,80,512]{2,1,0:T(8,128)(2,1)}, u32[]{:S(2)}, u32[]{:S(2)}) collective-permute-start(bf16[2,80,512]{2,1,0:T(8,128)(2,1)S(1)} %collective-permute-done.2.refs_2_), channel_id=1, source_target_pairs={{0,72},{8,0},{64,8},{72,64},{1,73},{9,1},{65,9},{73,65},{2,74},{10... | collective-permute-start | bytes 491528 | tf_op jit(solution)/shard_map/ppermute | solution.py:405
  39.4 3.7 %copy-start.16 = (bf16[2,80,512]{2,1,0:T(8,128)(2,1)}, bf16[2,80,512]{2,1,0:T(8,128)(2,1)S(1)}, u32[]{:S(2)}) copy-start(bf16[2,80,512]{2,1,0:T(8,128)(2,1)S(1)} %collective-permute-done.3.refs_3_) | copy-start | bytes 491524
  39.4 7.0 %collective-permute-start.7 = (bf16[2,80,512]{2,1,0:T(8,128)(2,1)S(1)}, bf16[2,80,512]{2,1,0:T(8,128)(2,1)}, u32[]{:S(2)}, u32[]{:S(2)}) collective-permute-start(bf16[2,80,512]{2,1,0:T(8,128)(2,1)S(1)} %collective-permute-done.3.refs_3_), channel_id=1, source_target_pairs={{0,72},{8,0},{64,8},{72,64},{1,73},{9,1},{65,9},{73,65},{2,74},{10... | collective-permute-start | bytes 491528 | tf_op jit(solution)/shard_map/ppermute | solution.py:405
  51.3 4.9 %copy-start.32 = (f32[512,128]{1,0:T(8,128)S(1)}, f32[512,128]{1,0:T(8,128)}, u32[]{:S(2)}) copy-start(f32[512,128]{1,0:T(8,128)} %get-tuple-element.84) | copy-start | bytes 786436
  51.3 6.8 %copy-start.31 = (f32[512,128]{1,0:T(8,128)S(1)}, f32[512,128]{1,0:T(8,128)}, u32[]{:S(2)}) copy-start(f32[512,128]{1,0:T(8,128)} %get-tuple-element.85) | copy-start | bytes 786436
  51.3 9.5 %copy-start.30 = (f32[512,128]{1,0:T(8,128)S(1)}, f32[512,128]{1,0:T(8,128)}, u32[]{:S(2)}) copy-start(f32[512,128]{1,0:T(8,128)} %get-tuple-element.86) | copy-start | bytes 786436
  51.3 43.0 %copy-start.13 = (f32[512,128]{1,0:T(8,128)S(1)}, f32[512,128]{1,0:T(8,128)}, u32[]{:S(2)}) copy-start(f32[512,128]{1,0:T(8,128)} %get-tuple-element.83) | copy-start | bytes 786436
  51.3 51.9 %copy-start.29 = (bf16[2,80,1024]{2,1,0:T(8,128)(2,1)S(1)}, bf16[2,80,1024]{2,1,0:T(8,128)(2,1)}, u32[]{:S(2)}) copy-start(bf16[2,80,1024]{2,1,0:T(8,128)(2,1)} %get-tuple-element.82) | copy-start | bytes 983044
  51.3 55.4 %all-to-all-start.1 = ((bf16[32,256,128]{2,1,0:T(8,128)(2,1)}), bf16[32,256,128]{2,1,0:T(8,128)(2,1)S(1)}, u32[]{:S(2)}, u32[]{:S(2)}) async-start(bf16[32,256,128]{2,1,0:T(8,128)(2,1)} %pack_cache.1), calls=%async_computation.1 | async-start | bytes 4194304 | tf_op jit(solution)/shard_map/all_to_all | solution.py:417
  56.2 32.5 %collective-permute-start.13 = (f32[512,128]{1,0:T(8,128)S(1)}, f32[512,128]{1,0:T(8,128)S(1)}, u32[]{:S(2)}, u32[]{:S(2)}) collective-permute-start(f32[512,128]{1,0:T(8,128)S(1)} %copy-done.32), channel_id=1, source_target_pairs={{0,16},{16,32},{32,48},{48,0},{1,17},{17,33},{33,49},{49,1},{2,18}... | collective-permute-start | bytes 786440 | tf_op jit(solution)/shard_map/ppermute | solution.py:409
  58.1 36.2 %collective-permute-start.14 = (f32[512,128]{1,0:T(8,128)S(1)}, f32[512,128]{1,0:T(8,128)S(1)}, u32[]{:S(2)}, u32[]{:S(2)}) collective-permute-start(f32[512,128]{1,0:T(8,128)S(1)} %copy-done.31), channel_id=1, source_target_pairs={{0,32},{16,48},{32,0},{48,16},{1,33},{17,49},{33,1},{49,17},{2,34}... | collective-permute-start | bytes 786440 | tf_op jit(solution)/shard_map/ppermute | solution.py:409
  60.8 33.5 %collective-permute-start.15 = (f32[512,128]{1,0:T(8,128)S(1)}, f32[512,128]{1,0:T(8,128)S(1)}, u32[]{:S(2)}, u32[]{:S(2)}) collective-permute-start(f32[512,128]{1,0:T(8,128)S(1)} %copy-done.30), channel_id=1, source_target_pairs={{0,48},{16,0},{32,16},{48,32},{1,49},{17,1},{33,17},{49,33},{2,50}... | collective-permute-start | bytes 786440 | tf_op jit(solution)/shard_map/ppermute | solution.py:409
  94.4 12.3 %copy-start.22 = (bf16[512,128]{1,0:T(8,128)(2,1)}, bf16[512,128]{1,0:T(8,128)(2,1)S(1)}, u32[]{:S(2)}) copy-start(bf16[512,128]{1,0:T(8,128)(2,1)S(1)} %add_convert_fusion.refs_0_) | copy-start | bytes 393220
  94.4 8.8 %collective-permute-start.18 = (bf16[512,128]{1,0:T(8,128)(2,1)S(1)}, bf16[512,128]{1,0:T(8,128)(2,1)}, u32[]{:S(2)}, u32[]{:S(2)}) collective-permute-start(bf16[512,128]{1,0:T(8,128)(2,1)S(1)} %add_convert_fusion.refs_0_), channel_id=1, source_target_pairs={{0,72},{8,0},{64,8},{72,64},{1,73},{9,1},{65,9},{73,65},{2,74},{10... | collective-permute-start | bytes 393224 | tf_op jit(solution)/shard_map/ppermute | solution.py:405
  97.9 8.2 %collective-permute-start.17 = (bf16[512,128]{1,0:T(8,128)(2,1)S(1)}, bf16[512,128]{1,0:T(8,128)(2,1)}, u32[]{:S(2)}, u32[]{:S(2)}) collective-permute-start(bf16[512,128]{1,0:T(8,128)(2,1)S(1)} %add_convert_fusion.refs_0_), channel_id=1, source_target_pairs={{0,64},{8,72},{64,0},{72,8},{1,65},{9,73},{65,1},{73,9},{2,66},{10... | collective-permute-start | bytes 393224 | tf_op jit(solution)/shard_map/ppermute | solution.py:405
  98.2 8.6 %collective-permute-start.16 = (bf16[512,128]{1,0:T(8,128)(2,1)S(1)}, bf16[512,128]{1,0:T(8,128)(2,1)}, u32[]{:S(2)}, u32[]{:S(2)}) collective-permute-start(bf16[512,128]{1,0:T(8,128)(2,1)S(1)} %add_convert_fusion.refs_0_), channel_id=1, source_target_pairs={{0,8},{8,64},{64,72},{72,0},{1,9},{9,65},{65,73},{73,1},{2,10},{10... | collective-permute-start | bytes 393224 | tf_op jit(solution)/shard_map/ppermute | solution.py:405
  98.9 26.0 %collective-permute-start.10 = (bf16[2,80,1024]{2,1,0:T(8,128)(2,1)}, bf16[2,80,1024]{2,1,0:T(8,128)(2,1)S(1)}, u32[]{:S(2)}, u32[]{:S(2)}) collective-permute-start(bf16[2,80,1024]{2,1,0:T(8,128)(2,1)} %get-tuple-element.80), channel_id=1, source_target_pairs={{0,2},{2,4},{4,6},{6,0},{1,3},{3,5},{5,7},{7,1},{8,10},{10,12},{12... | collective-permute-start | bytes 983048 | tf_op jit(solution)/shard_map/ppermute | solution.py:409
  100.4 24.6 %collective-permute-start.11 = (bf16[2,80,1024]{2,1,0:T(8,128)(2,1)}, bf16[2,80,1024]{2,1,0:T(8,128)(2,1)S(1)}, u32[]{:S(2)}, u32[]{:S(2)}) collective-permute-start(bf16[2,80,1024]{2,1,0:T(8,128)(2,1)} %get-tuple-element.81), channel_id=1, source_target_pairs={{0,4},{2,6},{4,0},{6,2},{1,5},{3,7},{5,1},{7,3},{8,12},{10,14},{12... | collective-permute-start | bytes 983048 | tf_op jit(solution)/shard_map/ppermute | solution.py:409
  103.2 21.7 %collective-permute-start.12 = (bf16[2,80,1024]{2,1,0:T(8,128)(2,1)S(1)}, bf16[2,80,1024]{2,1,0:T(8,128)(2,1)S(1)}, u32[]{:S(2)}, u32[]{:S(2)}) collective-permute-start(bf16[2,80,1024]{2,1,0:T(8,128)(2,1)S(1)} %copy-done.29), channel_id=1, source_target_pairs={{0,6},{2,0},{4,2},{6,4},{1,7},{3,1},{5,3},{7,5},{8,14},{10,8},{12,... | collective-permute-start | bytes 983048 | tf_op jit(solution)/shard_map/ppermute | solution.py:409
  124.9 4.0 %copy-start.7 = (bf16[8,272,128]{2,1,0:T(8,128)(2,1)S(1)}, bf16[8,272,128]{2,1,0:T(8,128)(2,1)}, u32[]{:S(2)}) copy-start(bf16[8,272,128]{2,1,0:T(8,128)(2,1)} %attend.1) | copy-start | bytes 1671172
  128.9 27.2 %collective-permute-start.22 = (bf16[640,1024]{1,0:T(8,128)(2,1)}, bf16[640,1024]{1,0:T(8,128)(2,1)S(1)}, u32[]{:S(2)}, u32[]{:S(2)}) collective-permute-start(bf16[640,1024]{1,0:T(8,128)(2,1)} %settle.1.refs_4_), channel_id=1, source_target_pairs={{0,1},{1,0},{2,3},{3,2},{4,5},{5,4},{6,7},{7,6},{8,9},{9,8},{10,11... | collective-permute-start | bytes 3932168 | tf_op jit(solution)/shard_map/ppermute | solution.py:413
  146.2 6.6 %collective-permute-start.21 = (bf16[256,256]{1,0:T(8,128)(2,1)}, bf16[256,256]{1,0:T(8,128)(2,1)S(1)}, u32[]{:S(2)}, u32[]{:S(2)}) collective-permute-start(bf16[256,256]{1,0:T(8,128)(2,1)} %merge.1.refs_0_), channel_id=1, source_target_pairs={{0,48},{16,0},{32,16},{48,32},{1,49},{17,1},{33,17},{49,33},{2,50}... | collective-permute-start | bytes 393224 | tf_op jit(solution)/shard_map/ppermute | solution.py:409
  146.4 7.6 %collective-permute-start.20 = (bf16[256,256]{1,0:T(8,128)(2,1)}, bf16[256,256]{1,0:T(8,128)(2,1)S(1)}, u32[]{:S(2)}, u32[]{:S(2)}) collective-permute-start(bf16[256,256]{1,0:T(8,128)(2,1)} %merge.1.refs_0_), channel_id=1, source_target_pairs={{0,32},{16,48},{32,0},{48,16},{1,33},{17,49},{33,1},{49,17},{2,34}... | collective-permute-start | bytes 393224 | tf_op jit(solution)/shard_map/ppermute | solution.py:409
  148.5 7.6 %collective-permute-start.19 = (bf16[256,256]{1,0:T(8,128)(2,1)}, bf16[256,256]{1,0:T(8,128)(2,1)S(1)}, u32[]{:S(2)}, u32[]{:S(2)}) collective-permute-start(bf16[256,256]{1,0:T(8,128)(2,1)} %merge.1.refs_0_), channel_id=1, source_target_pairs={{0,16},{16,32},{32,48},{48,0},{1,17},{17,33},{33,49},{49,1},{2,18}... | collective-permute-start | bytes 393224 | tf_op jit(solution)/shard_map/ppermute | solution.py:409
  152.8 3.3 %copy-start.23 = (bf16[256,256]{1,0:T(8,128)(2,1)}, bf16[256,256]{1,0:T(8,128)(2,1)S(1)}, u32[]{:S(2)}) copy-start(bf16[256,256]{1,0:T(8,128)(2,1)S(1)} %collective-permute-done.21.refs_3_) | copy-start | bytes 393220
  154.0 2.1 %copy-start.24 = (bf16[256,256]{1,0:T(8,128)(2,1)}, bf16[256,256]{1,0:T(8,128)(2,1)S(1)}, u32[]{:S(2)}) copy-start(bf16[256,256]{1,0:T(8,128)(2,1)S(1)} %collective-permute-done.20.refs_2_) | copy-start | bytes 393220
  162.0 10.7 %collective-permute-start.23 = (bf16[64,1280]{1,0:T(8,128)(2,1)}, bf16[64,1280]{1,0:T(8,128)(2,1)S(1)}, u32[]{:S(2)}, u32[]{:S(2)}) collective-permute-start(bf16[64,1280]{1,0:T(8,128)(2,1)} %get-tuple-element.94), channel_id=1, source_target_pairs={{0,2},{2,4},{4,6},{6,0},{1,3},{3,5},{5,7},{7,1},{8,10},{10,12},{12... | collective-permute-start | bytes 491528 | tf_op jit(solution)/shard_map/ppermute | solution.py:409
  162.4 10.2 %collective-permute-start.24 = (bf16[64,1280]{1,0:T(8,128)(2,1)}, bf16[64,1280]{1,0:T(8,128)(2,1)S(1)}, u32[]{:S(2)}, u32[]{:S(2)}) collective-permute-start(bf16[64,1280]{1,0:T(8,128)(2,1)} %get-tuple-element.95), channel_id=1, source_target_pairs={{0,4},{2,6},{4,0},{6,2},{1,5},{3,7},{5,1},{7,3},{8,12},{10,14},{12... | collective-permute-start | bytes 491528 | tf_op jit(solution)/shard_map/ppermute | solution.py:409
  165.0 8.2 %collective-permute-start.25 = (bf16[64,1280]{1,0:T(8,128)(2,1)}, bf16[64,1280]{1,0:T(8,128)(2,1)S(1)}, u32[]{:S(2)}, u32[]{:S(2)}) collective-permute-start(bf16[64,1280]{1,0:T(8,128)(2,1)} %get-tuple-element.96), channel_id=1, source_target_pairs={{0,6},{2,0},{4,2},{6,4},{1,7},{3,1},{5,3},{7,5},{8,14},{10,8},{12,... | collective-permute-start | bytes 491528 | tf_op jit(solution)/shard_map/ppermute | solution.py:409
  175.9 5.4 %collective-permute-start.26 = (bf16[16,1280]{1,0:T(8,128)(2,1)}, bf16[16,1280]{1,0:T(8,128)(2,1)S(1)}, u32[]{:S(2)}, u32[]{:S(2)}) collective-permute-start(bf16[16,1280]{1,0:T(8,128)(2,1)} %get-tuple-element.98), channel_id=1, source_target_pairs={{0,16},{16,32},{32,48},{48,0},{1,17},{17,33},{33,49},{49,1},{2,18}... | collective-permute-start | bytes 122888 | tf_op jit(solution)/shard_map/ppermute | solution.py:409
  175.9 5.9 %collective-permute-start.27 = (bf16[16,1280]{1,0:T(8,128)(2,1)}, bf16[16,1280]{1,0:T(8,128)(2,1)S(1)}, u32[]{:S(2)}, u32[]{:S(2)}) collective-permute-start(bf16[16,1280]{1,0:T(8,128)(2,1)} %get-tuple-element.99), channel_id=1, source_target_pairs={{0,32},{16,48},{32,0},{48,16},{1,33},{17,49},{33,1},{49,17},{2,34}... | collective-permute-start | bytes 122888 | tf_op jit(solution)/shard_map/ppermute | solution.py:409
  178.0 4.6 %collective-permute-start.28 = (bf16[16,1280]{1,0:T(8,128)(2,1)}, bf16[16,1280]{1,0:T(8,128)(2,1)S(1)}, u32[]{:S(2)}, u32[]{:S(2)}) collective-permute-start(bf16[16,1280]{1,0:T(8,128)(2,1)} %get-tuple-element.100), channel_id=1, source_target_pairs={{0,48},{16,0},{32,16},{48,32},{1,49},{17,1},{33,17},{49,33},{2,50}... | collective-permute-start | bytes 122888 | tf_op jit(solution)/shard_map/ppermute | solution.py:409
  (16 other events, 13.4 us)

commit v2 on v1

--- a/solution.py
+++ b/solution.py
@@ -13,7 +13,7 @@
 HEADS = 32
 BLOCK = 128
 KEY_TILES = 32
-GROUP = 8
+GROUP = 16
 Q_DEV = 16
 NEG = -1e30
 AXES = ("tm", "y", "zl", "x", "c")
@@ -178,42 +178,27 @@
 
 
 def project_kernel(place_ref, *refs):
-    rows, weights, outs, (w_ref, total_ref) = refs[:4], refs[4:6], refs[6:10], refs[10:]
-    y, x, core = place_ref[0], place_ref[1], place_ref[2]
-    size = weights[0].shape[0] // 8
-    for side in range(2):
-        for pair in range(8):
-            block = pair * 2 + lax.rem(core + side, 2)
-            target = pl.ds(pl.multiple_of(block * size, 16), size)
-            w_ref[target, :] = weights[side][pl.ds(pair * size, size), :]
+    rows, w_ref, out_ref = refs[:4], refs[4], refs[5]
     total = None
     for s in range(4):
-        source = lax.rem(y - s + 4, 4)
+        source = lax.rem(place_ref[0] - s + 4, 4)
         w = w_ref[:, pl.ds(pl.multiple_of(source * 256, 256), 256)]
         term = lax.dot_general(rows[s][...], w, NT, preferred_element_type=jnp.float32)
         total = term if total is None else total + term
-    total_ref[...] = total
-    for s in range(4):
-        target = lax.rem(x + s, 4)
-        for i in range(4):
-            start = pl.multiple_of(i * 64 + target * 16, 16)
-            outs[s][pl.ds(i * 16, 16), :] = total_ref[pl.ds(start, 16), :].astype(outs[s].dtype)
+    for target in range(16):
+        out_ref[target] = total[target * Q_DEV : (target + 1) * Q_DEV].astype(jnp.bfloat16)
 
 
 def project(place, rows, weights):
     vmem = pl.BlockSpec(memory_space=pltpu.VMEM)
-    kinds = [jnp.float32] + [jnp.bfloat16] * 3
+    width = weights.shape[0]
     return pl.pallas_call(
         project_kernel,
-        out_shape=tuple(jax.ShapeDtypeStruct((64, 1280), kind) for kind in kinds),
-        in_specs=[pl.BlockSpec(memory_space=pltpu.SMEM)] + [vmem] * 6,
-        out_specs=(vmem,) * 4,
-        scratch_shapes=[
-            pltpu.VMEM((1280, 8 * HD), jnp.bfloat16),
-            pltpu.VMEM((256, 1280), jnp.float32),
-        ],
+        out_shape=jax.ShapeDtypeStruct((16, Q_DEV, width), jnp.bfloat16),
+        in_specs=[pl.BlockSpec(memory_space=pltpu.SMEM)] + [vmem] * 5,
+        out_specs=vmem,
         name="project",
-    )(place, *rows, *weights)
+    )(place, *rows, weights)
 
 
 def pack_query_kernel(place_ref, near_ref, far_ref, *out_refs):
@@ -274,99 +259,70 @@
 
 
 def settle_kernel(place_ref, *refs):
-    parts, out_ref = refs[:4], refs[4]
-    x = place_ref[1]
-    size = parts[0].shape[1]
-    for side in range(2):
+    parts, out_ref = refs[:8], refs[8]
+    x, zl = place_ref[1], place_ref[3]
+    size = parts[0].shape[0]
+    for z_side in range(2):
         for s in range(4):
-            block = side * 4 + lax.rem(x - s + 4, 4)
-            out_ref[pl.ds(pl.multiple_of(block * size, 16), size), :] = parts[s][side]
+            block = lax.rem(zl + z_side, 2) * 4 + lax.rem(x - s + 4, 4)
+            out_ref[pl.ds(pl.multiple_of(block * size, 16), size), :] = parts[z_side * 4 + s][...]
 
 
 def settle(place, parts):
     vmem = pl.BlockSpec(memory_space=pltpu.VMEM)
-    _, rows, columns = parts[0].shape
+    rows, columns = parts[0].shape
     return pl.pallas_call(
         settle_kernel,
         out_shape=jax.ShapeDtypeStruct((8 * rows, columns), jnp.bfloat16),
-        in_specs=[pl.BlockSpec(memory_space=pltpu.SMEM)] + [vmem] * 4,
+        in_specs=[pl.BlockSpec(memory_space=pltpu.SMEM)] + [vmem] * 8,
         out_specs=vmem,
         name="settle",
     )(place, *parts)
 
 
-def finish_kernel(place_ref, *refs):
-    parts, out_ref = refs[:4], refs[4]
-    width = parts[0].shape[1]
-    for s in range(4):
-        source = lax.rem(place_ref[0] - s + 4, 4)
-        columns = pl.ds(pl.multiple_of(source * width, HD), width)
-        out_ref[:, columns] = parts[s][...]
-
-
-def finish(place, parts):
-    vmem = pl.BlockSpec(memory_space=pltpu.VMEM)
-    rows, width = parts[0].shape
+def finish_kernel(part_ref, out_ref):
+    width = part_ref.shape[2]
+    for y in range(4):
+        parts = [part_ref[y * 4 + x].astype(jnp.float32) for x in range(4)]
+        total = functools.reduce(jnp.add, parts)
+        out_ref[:, y * width : (y + 1) * width] = total.astype(jnp.bfloat16)
+
+
+def finish(parts):
+    vmem = pl.BlockSpec(memory_space=pltpu.VMEM)
+    _, rows, width = parts.shape
     return pl.pallas_call(
         finish_kernel,
         out_shape=jax.ShapeDtypeStruct((rows, 4 * width), jnp.bfloat16),
-        in_specs=[pl.BlockSpec(memory_space=pltpu.SMEM)] + [vmem] * 4,
+        in_specs=[vmem],
         out_specs=vmem,
         name="finish",
-    )(place, *parts)
-
-
-def add_kernel(place_ref, *refs):
-    parts, outs, total_ref = refs[:4], refs[4:8], refs[8]
-    total = parts[0][...]
-    for part in parts[1:]:
-        total = total + part[...].astype(jnp.float32)
-    total_ref[...] = total
+    )(parts)
+
+
+def pack_out_kernel(place_ref, w_ref, *out_refs):
+    x = place_ref[1]
     for s in range(4):
-        start = pl.multiple_of(lax.rem(place_ref[0] + s, 4) * Q_DEV, Q_DEV)
-        outs[s][...] = total_ref[pl.ds(start, Q_DEV), :].astype(jnp.bfloat16)
-
-
-def add_parts(place, parts):
-    vmem = pl.BlockSpec(memory_space=pltpu.VMEM)
-    rows, width = parts[0].shape
-    return pl.pallas_call(
-        add_kernel,
-        out_shape=(jax.ShapeDtypeStruct((Q_DEV, width), jnp.bfloat16),) * 4,
-        in_specs=[pl.BlockSpec(memory_space=pltpu.SMEM)] + [vmem] * 4,
-        out_specs=(vmem,) * 4,
-        scratch_shapes=[pltpu.VMEM((rows, width), jnp.float32)],
-        name="add_parts",
-    )(place, *parts)
-
-
-def pack_out_kernel(place_ref, *refs):
-    x, zl = place_ref[1], place_ref[3]
-    halves, out_refs = refs[:4], refs[4:]
-    for s in range(4):
-        for z_side in range(2):
-            side = lax.rem(zl + z_side, 2)
-            for y in range(4):
-                head = y % 2 * 8 + lax.rem(x + s, 4) * 2
-                columns = pl.ds(pl.multiple_of(head * HD, 2 * HD), 2 * HD)
-                block = halves[z_side * 2 + y // 2][:, columns]
-                out_refs[s][side, :, y * 2 * HD : (y + 1) * 2 * HD] = block
-
-
-def pack_out(place, halves):
-    vmem = pl.BlockSpec(memory_space=pltpu.VMEM)
-    rows = halves[0].shape[0]
+        for y in range(4):
+            head = y * 8 + lax.rem(x + s, 4) * 2
+            columns = pl.ds(pl.multiple_of(head * HD, 2 * HD), 2 * HD)
+            out_refs[s][:, y * 2 * HD : (y + 1) * 2 * HD] = w_ref[:, columns]
+
+
+def pack_out(place, table):
+    vmem = pl.BlockSpec(memory_space=pltpu.VMEM)
+    rows = table.shape[0]
     return pl.pallas_call(
         pack_out_kernel,
-        out_shape=(jax.ShapeDtypeStruct((2, rows, 8 * HD), jnp.bfloat16),) * 4,
-        in_specs=[pl.BlockSpec(memory_space=pltpu.SMEM)] + [vmem] * 4,
+        out_shape=(jax.ShapeDtypeStruct((rows, 8 * HD), jnp.bfloat16),) * 4,
+        in_specs=[pl.BlockSpec(memory_space=pltpu.SMEM), vmem],
         out_specs=(vmem,) * 4,
         name="pack_out",
-    )(place, *halves)
-
-
-def query_kernel(place_ref, token_ref, *refs):
-    weights, out_refs, (w_ref, total_ref) = refs[:8], refs[8:12], refs[12:]
+    )(place, table)
+
+
+def weave_query_kernel(place_ref, *refs):
+    weights, out_ref = refs[:8], refs[8]
     y, x, core, zl = place_ref[0], place_ref[1], place_ref[2], place_ref[3]
     size = weights[0].shape[1]
     for z_side in range(2):
@@ -375,30 +331,68 @@
                 block = lax.rem(zl + z_side, 2) * 8 + lax.rem(x - s + 4, 4) * 2
                 block = block + lax.rem(core + side, 2)
                 rows = pl.ds(pl.multiple_of(block * size, 16), size)
-                w_ref[rows, :] = weights[z_side * 4 + s][side]
-    total_ref[...] = jnp.dot(token_ref[...], w_ref[...], preferred_element_type=jnp.float32)
-    for s in range(4):
-        columns = pl.ds(pl.multiple_of(lax.rem(y + s, 4) * HD, HD), HD)
-        out_refs[s][...] = total_ref[:, columns]
-
-
-def query_parts(place, token_rows, weights):
+                for t in range(4):
+                    columns = pl.ds(pl.multiple_of(lax.rem(y + t, 4) * HD, HD), HD)
+                    block = weights[z_side * 4 + s][side, :, columns]
+                    out_ref[rows, t * HD : (t + 1) * HD] = block
+
+
+def weave_query(place, weights):
+    vmem = pl.BlockSpec(memory_space=pltpu.VMEM)
+    _, rows, columns = weights[0].shape
+    return pl.pallas_call(
+        weave_query_kernel,
+        out_shape=jax.ShapeDtypeStruct((16 * rows, columns), jnp.bfloat16),
+        in_specs=[pl.BlockSpec(memory_space=pltpu.SMEM)] + [vmem] * 8,
+        out_specs=vmem,
+        name="weave_query",
+    )(place, *weights)
+
+
+def weave_out_kernel(place_ref, *refs):
+    weights, out_ref = refs[:2], refs[2]
+    core = place_ref[2]
+    size = weights[0].shape[0] // 8
+    for side in range(2):
+        for pair in range(8):
+            block = pair * 2 + lax.rem(core + side, 2)
+            target = pl.ds(pl.multiple_of(block * size, 16), size)
+            out_ref[target, :] = weights[side][pl.ds(pair * size, size), :]
+
+
+def weave_out(place, weights):
+    vmem = pl.BlockSpec(memory_space=pltpu.VMEM)
+    rows, columns = weights[0].shape
+    return pl.pallas_call(
+        weave_out_kernel,
+        out_shape=jax.ShapeDtypeStruct((2 * rows, columns), jnp.bfloat16),
+        in_specs=[pl.BlockSpec(memory_space=pltpu.SMEM)] + [vmem] * 2,
+        out_specs=vmem,
+        name="weave_out",
+    )(place, *weights)
+
+
+def query_kernel(token_ref, w_ref, *out_refs):
+    for pair in range(2):
+        w = w_ref[:, pair * 2 * HD : (pair + 1) * 2 * HD]
+        total = jnp.dot(token_ref[...], w, preferred_element_type=jnp.float32)
+        out_refs[2 * pair][...] = total[:, :HD]
+        out_refs[2 * pair + 1][...] = total[:, HD:]
+
+
+def query_parts(token_rows, weights):
     vmem = pl.BlockSpec(memory_space=pltpu.VMEM)
     rows, depth = token_rows.shape
     return pl.pallas_call(
         query_kernel,
         out_shape=(jax.ShapeDtypeStruct((rows, HD), jnp.float32),) * 4,
-        in_specs=[pl.BlockSpec(memory_space=pltpu.SMEM)] + [vmem] * 9,
+        in_specs=[vmem] * 2,
         out_specs=(vmem,) * 4,
-        scratch_shapes=[
-            pltpu.VMEM((depth, 4 * HD), jnp.bfloat16),
-            pltpu.VMEM((rows, 4 * HD), jnp.float32),
-        ],
         cost_estimate=pl.CostEstimate(
             flops=2 * rows * depth * 4 * HD, bytes_accessed=4 * 2**20, transcendentals=0
         ),
         name="query_parts",
-    )(place, token_rows, *weights)
+    )(token_rows, weights)
 
 
 def z_shift(value, shift):
@@ -428,34 +422,33 @@
 
     token_rows = exchange(pack_tokens(tokens), PLANE)
 
-    half = w_out.shape[0] // 2
-    low, high = w_out[:half].T, w_out[half:].T
-    packed_out = pack_out(place, (low, high, z_shift(low, 1), z_shift(high, -1)))
+    packed_out = pack_out(place, w_out.T)
+    got_out = [packed_out[0]] + [ring_shift(packed_out[s], "x", s) for s in (1, 2, 3)]
+
     cache = pack_cache(k_cache, v_cache)
-    ready = lax.optimization_barrier((weights, packed_out, cache, token_rows))
-    weights, packed_out, cache, token_rows = ready
-
-    partial = query_parts(place, token_rows.reshape(-1, token_rows.shape[2]), weights)
-    partial, cache, packed_out = lax.optimization_barrier((partial, cache, packed_out))
+    weights = weave_query(place, weights)
+    weights, cache, token_rows = lax.optimization_barrier((weights, cache, token_rows))
+
+    partial = query_parts(token_rows.reshape(-1, token_rows.shape[2]), weights)
+    partial, cache, got_out = lax.optimization_barrier((partial, cache, got_out))
     partial = [partial[0]] + [ring_shift(partial[s], "y", s) for s in (1, 2, 3)]
     arrived = exchange(cache, PLANE)
-    got = [packed_out[0]] + [ring_shift(packed_out[s], "x", s) for s in (1, 2, 3)]
+    got_out = list(got_out)
+    got_out += [z_shift(got_out[s], 1) for s in (0, 1)]
+    got_out += [z_shift(got_out[s], -1) for s in (2, 3)]
 
     query = functools.reduce(jnp.add, partial).astype(jnp.bfloat16)
     queries = [query] + [z_shift(query, s) for s in (1, 2, 3)]
     outs = attend(plane, slot_frame, radial_mask, queries, arrived)
 
-    got, outs = lax.optimization_barrier((got, outs))
-    out_near = settle(place, got)
+    got_out, outs = lax.optimization_barrier((got_out, outs))
+    out_near = settle(place, got_out)
+    parts = exchange(outs, ("tm", "zl", "c"))
     out_far = core_swap(out_near)
-    parts = exchange(outs, ("tm", "zl", "c"))
+    out_weights = weave_out(place, (out_near, out_far))
     attended = merge(core, parts)
     rows = [attended] + [ring_shift(attended, "y", s) for s in (1, 2, 3)]
-    parts = project(place, rows, (out_near, out_far))
-    parts = [parts[0]] + [ring_shift(parts[s], "x", s) for s in (1, 2, 3)]
-    parts = add_parts(place, parts)
-    parts = [parts[0]] + [ring_shift(parts[s], "y", s) for s in (1, 2, 3)]
-    return finish(place, parts)
+    return finish(exchange(project(place, rows, out_weights), ("y", "x")))
 
 
 def solution(mesh):

time: 186 us -> 189 us (1.016)
  blocking collectives: 15.2 us -> 34.2 us
  starting transfers between devices: 59.2 us -> 49.7 us
  waiting for transfers between devices: 58.5 us -> 49.3 us
  Pallas kernels: 43 us -> 45 us
    all_to_all x1 -> x2, blocking collectives: 15.2 us -> 34.2 us  [exchange(): return lax.all_to_all(table, axes, split_axis=0, concat_axis=0, tiled=True)]
    ppermute x18 -> x12, waiting for transfers between devices: 57.7 us -> 44 us  [ring_shift(): return lax.ppermute(value, axis, [(i, (i + shift) % 4) for i in range(4)])]
    ppermute x18 -> x12, starting transfers between devices: 31.5 us -> 18.8 us  [ring_shift(): return lax.ppermute(value, axis, [(i, (i + shift) % 4) for i in range(4)])]
    pallas_call x3 -> x4, Pallas kernels: 8.63 us -> 12 us  [the longest x1 3.76 us: project(): pl.pallas_call(project_kernel, out_shape=jax.ShapeDtypeStruct((16, Q_DEV,...]
    ppermute x9 -> x11, waiting for transfers between devices: 0.77 us -> 4.13 us  [z_shift(): lax.ppermute(value, ('tm', 'zl'), [(i, (i + shift) % 4) for i in range(4)])]
    all_to_all x2, starting transfers between devices: 12.4 us -> 14.8 us  [exchange(): return lax.all_to_all(table, axes, split_axis=0, concat_axis=0, tiled=True)]
    ppermute x9 -> x11, starting transfers between devices: 15 us -> 15.7 us  [z_shift(): lax.ppermute(value, ('tm', 'zl'), [(i, (i + shift) % 4) for i in range(4)])]
    unnamed x66 -> x54, local copies, waits for them, and re-layouts: 7.78 us -> 7.93 us
  transfers between devices with their start and end apart: 31 -> 27, of which waited for: 14 -> 9; matrix products, arithmetic and copies ran while one was open for 0% -> 1% of each run, Pallas kernels for 15% -> 18%
where the time goes in v2:
time: 189 us; the launch traced here: 188 us
  starting transfers between devices  49.7 us (26%)
  waiting for transfers between devices  49.3 us (26%)
  Pallas kernels  45 us (24%)
  blocking collectives  34.2 us (18%)
  local copies, waits for them, and re-layouts  7.93 us (4%)
    ppermute x12, waiting for transfers between devices, ring_shift(): return lax.ppermute(value, axis, [(i, (i + shift) % 4) for i in range(4)])  44 us
    all_to_all x2, blocking collectives, exchange(): return lax.all_to_all(table, axes, split_axis=0, concat_axis=0, tiled=True)  34.2 us
    ppermute x12, starting transfers between devices, ring_shift(): return lax.ppermute(value, axis, [(i, (i + shift) % 4) for i in range(4)])  18.8 us
    ppermute x11, starting transfers between devices, z_shift(): lax.ppermute(value, ('tm', 'zl'), [(i, (i + shift) % 4) for i in range(4)])  15.7 us
    pallas_call x1, Pallas kernels, attend(): pl.pallas_call(attention_kernel, out_shape=jax.ShapeDtypeStruct((8, 272,...  15.3 us
    all_to_all x2, starting transfers between devices, exchange(): return lax.all_to_all(table, axes, split_axis=0, concat_axis=0, tiled=True)  14.8 us
    unnamed x54, local copies, waits for them, and re-layouts  7.93 us
    ppermute x11, waiting for transfers between devices, z_shift(): lax.ppermute(value, ('tm', 'zl'), [(i, (i + shift) % 4) for i in range(4)])  4.13 us
  transfers between devices with their start and end apart: 27, of which 9 were waited for; matrix products, arithmetic and copies ran while one was open for 1% of the time, Pallas kernels for 18%

profile of v2, /device:TPU:0, one launch (start us, length us, event | category | flops | bytes accessed | tf_op | source)
XLA Modules:
  0.0 187.8 jit_solution(18423350564387232904)
XLA Ops:
  0.0 2.1 %pack_tokens.1 = bf16[32,16,1280]{2,1,0:T(8,128)(2,1)} custom-call(bf16[16,5120]{1,0:T(8,128)(2,1)} %token_ref.1), custom_call_target="tpu_custom_call" | custom-call | tf_op jit(solution)/shard_map/pack_tokens/pallas_call | solution.py:252
  2.1 7.6 %all-to-all-start = ((bf16[32,16,1280]{2,1,0:T(8,128)(2,1)}), bf16[32,16,1280]{2,1,0:T(8,128)(2,1)S(1)}, u32[]{:S(2)}, u32[]{:S(2)}) async-start(bf16[32,16,1280]{2,1,0:T(8,128)(2,1)} %pack_tokens.1), calls=%async_computation | async-start | bytes 2621440 | tf_op jit(solution)/shard_map/all_to_all | solution.py:411
  10.0 0.7 pad_add_fusion.place_ref
  10.7 1.2 collective-permute-done.far_ref
  11.9 0.9 copy-done.4
  12.7 2.3 %pack_query.1 = (bf16[2,80,512]{2,1,0:T(8,128)(2,1)}, bf16[2,80,512]{2,1,0:T(8,128)(2,1)}, bf16[2,80,512]{2,1,0:T(8,128)(2,1)}, bf16[2,80,512]{2,1,0:T(8,128)(2,1)}) custom-call(s32[4]{0:T(128)} %pad_add_fusion.place_ref, bf16[80,4096]{1,0:T(8,128)(2,1)} %near_ref.1, bf16[80,4096]{1,0:T(8,128)(2,1)} %copy-done.4), custom_call_target="tpu_custom_call" | custom-call | tf_op jit(solution)/shard_map/pack_query/pallas_call | solution.py:217
  15.0 1.8 collective-permute-start.1
  16.8 2.7 %collective-permute-start.2 = (bf16[2,80,512]{2,1,0:T(8,128)(2,1)}, bf16[2,80,512]{2,1,0:T(8,128)(2,1)S(1)}, u32[]{:S(2)}, u32[]{:S(2)}) collective-permute-start(bf16[2,80,512]{2,1,0:T(8,128)(2,1)} %get-tuple-element.40), channel_id=1, source_target_pairs={{0,4},{2,6},{4,0},{6,2},{1,5},{3,7},{5,1},{7,3},{8,12},{10,14},{12... | collective-permute-start | bytes 491528 | tf_op jit(solution)/shard_map/ppermute | solution.py:403
  19.5 1.5 collective-permute-start.3
  20.9 1.9 %collective-permute-start.4 = (bf16[2,80,512]{2,1,0:T(8,128)(2,1)}, bf16[2,80,512]{2,1,0:T(8,128)(2,1)S(1)}, u32[]{:S(2)}, u32[]{:S(2)}) collective-permute-start(bf16[2,80,512]{2,1,0:T(8,128)(2,1)} %get-tuple-element.38.refs_0_), channel_id=1, source_target_pairs={{0,8},{8,64},{64,72},{72,0},{1,9},{9,65},{65,73},{73,1},{2,10},{10... | collective-permute-start | bytes 491528 | tf_op jit(solution)/shard_map/ppermute | solution.py:399
  22.8 8.5 %collective-permute-done.1.refs_1_ = bf16[2,80,512]{2,1,0:T(8,128)(2,1)S(1)} collective-permute-done((bf16[2,80,512]{2,1,0:T(8,128)(2,1)}, bf16[2,80,512]{2,1,0:T(8,128)(2,1)S(1)}, u32[]{:S(2)}, u32[]{:S(2)}) %collective-permute-start.1) | collective-permute-done | bytes 163872 | tf_op jit(solution)/shard_map/ppermute | solution.py:403
  31.3 1.9 %collective-permute-start.5 = (bf16[2,80,512]{2,1,0:T(8,128)(2,1)S(1)}, bf16[2,80,512]{2,1,0:T(8,128)(2,1)S(1)}, u32[]{:S(2)}, u32[]{:S(2)}) collective-permute-start(bf16[2,80,512]{2,1,0:T(8,128)(2,1)S(1)} %collective-permute-done.1.refs_1_), channel_id=1, source_target_pairs={{0,8},{8,64},{64,72},{72,0},{1,9},{9,65},{65,73},{73,1},{2,10},{10... | collective-permute-start | bytes 491528 | tf_op jit(solution)/shard_map/ppermute | solution.py:399
  33.2 2.1 %collective-permute-done.2.refs_2_ = bf16[2,80,512]{2,1,0:T(8,128)(2,1)S(1)} collective-permute-done((bf16[2,80,512]{2,1,0:T(8,128)(2,1)}, bf16[2,80,512]{2,1,0:T(8,128)(2,1)S(1)}, u32[]{:S(2)}, u32[]{:S(2)}) %collective-permute-start.2) | collective-permute-done | bytes 163872 | tf_op jit(solution)/shard_map/ppermute | solution.py:403
  35.3 4.0 %collective-permute-start.6 = (bf16[2,80,512]{2,1,0:T(8,128)(2,1)S(1)}, bf16[2,80,512]{2,1,0:T(8,128)(2,1)S(1)}, u32[]{:S(2)}, u32[]{:S(2)}) collective-permute-start(bf16[2,80,512]{2,1,0:T(8,128)(2,1)S(1)} %collective-permute-done.2.refs_2_), channel_id=1, source_target_pairs={{0,72},{8,0},{64,8},{72,64},{1,73},{9,1},{65,9},{73,65},{2,74},{10... | collective-permute-start | bytes 491528 | tf_op jit(solution)/shard_map/ppermute | solution.py:399
  39.8 2.1 %pack_out.1 = (bf16[80,1024]{1,0:T(8,128)(2,1)}, bf16[80,1024]{1,0:T(8,128)(2,1)}, bf16[80,1024]{1,0:T(8,128)(2,1)}, bf16[80,1024]{1,0:T(8,128)(2,1)}) custom-call(s32[4]{0:T(128)} %pad_add_fusion.place_ref, bf16[80,4096]{1,0:T(8,128)(2,1)} %bitcast.8), custom_call_target="tpu_custom_call" | custom-call | tf_op jit(solution)/shard_map/pack_out/pallas_call | solution.py:315
  41.9 2.0 %collective-permute-start.8 = (bf16[80,1024]{1,0:T(8,128)(2,1)}, bf16[80,1024]{1,0:T(8,128)(2,1)S(1)}, u32[]{:S(2)}, u32[]{:S(2)}) collective-permute-start(bf16[80,1024]{1,0:T(8,128)(2,1)} %get-tuple-element.50), channel_id=1, source_target_pairs={{0,2},{2,4},{4,6},{6,0},{1,3},{3,5},{5,7},{7,1},{8,10},{10,12},{12... | collective-permute-start | bytes 491528 | tf_op jit(solution)/shard_map/ppermute | solution.py:403
  44.4 3.2 %pack_cache.1 = bf16[32,256,128]{2,1,0:T(8,128)(2,1)} custom-call(bf16[128,4096]{1,0:T(8,128)(2,1)} %k_ref.1, bf16[128,4096]{1,0:T(8,128)(2,1)} %v_ref.1), custom_call_target="tpu_custom_call" | custom-call | tf_op jit(solution)/shard_map/pack_cache/pallas_call | solution.py:234
  48.4 0.7 copy-done.20
  49.1 2.8 %weave_query.1.w_ref = bf16[1280,512]{1,0:T(8,128)(2,1)} custom-call(s32[4]{0:T(128)} %pad_add_fusion.place_ref, bf16[2,80,512]{2,1,0:T(8,128)(2,1)} %get-tuple-element.38.refs_0_, bf16[2,80,512]{2,1,0:T(8,128)(2,1)} %copy-done.11, bf16[2,80,512]{2,1,0:T(8,128)(2,1)} %copy-done.12, bf16[2,80,512]{2,1,0:T(8,128)(2,1)} %copy-done.13, ...), custom_call_target="tpu_custom_call" | custom-call | tf_op jit(solution)/shard_map/weave_query/pallas_call | solution.py:343
  51.9 1.1 copy-done
  53.0 3.5 %query_parts.1 = (f32[512,128]{1,0:T(8,128)}, f32[512,128]{1,0:T(8,128)}, f32[512,128]{1,0:T(8,128)}, f32[512,128]{1,0:T(8,128)}) custom-call(bf16[512,1280]{1,0:T(8,128)(2,1)} %bitcast.7, bf16[1280,512]{1,0:T(8,128)(2,1)} %weave_query.1.w_ref), custom_call_target="tpu_custom_call" | custom-call | flops 671088640 | bytes 4194304 | tf_op jit(solution)/shard_map/query_parts/pallas_call | solution.py:386
  56.6 7.3 %all-to-all-start.1 = ((bf16[32,256,128]{2,1,0:T(8,128)(2,1)}), bf16[32,256,128]{2,1,0:T(8,128)(2,1)S(1)}, u32[]{:S(2)}, u32[]{:S(2)}) async-start(bf16[32,256,128]{2,1,0:T(8,128)(2,1)} %pack_cache.1), calls=%async_computation.1 | async-start | bytes 4194304 | tf_op jit(solution)/shard_map/all_to_all | solution.py:411
  63.9 1.9 collective-permute-start.15
  65.8 2.7 %collective-permute-start.16 = (f32[512,128]{1,0:T(8,128)S(1)}, f32[512,128]{1,0:T(8,128)S(1)}, u32[]{:S(2)}, u32[]{:S(2)}) collective-permute-start(f32[512,128]{1,0:T(8,128)S(1)} %copy-done.26), channel_id=1, source_target_pairs={{0,32},{16,48},{32,0},{48,16},{1,33},{17,49},{33,1},{49,17},{2,34}... | collective-permute-start | bytes 786440 | tf_op jit(solution)/shard_map/ppermute | solution.py:403
  68.5 1.4 collective-permute-start.17
  69.9 26.5 %collective-permute-done.15 = f32[512,128]{1,0:T(8,128)S(1)} collective-permute-done((f32[512,128]{1,0:T(8,128)}, f32[512,128]{1,0:T(8,128)S(1)}, u32[]{:S(2)}, u32[]{:S(2)}) %collective-permute-start.15) | collective-permute-done | bytes 262176 | tf_op jit(solution)/shard_map/ppermute | solution.py:403
  96.4 5.6 %collective-permute-done.16 = f32[512,128]{1,0:T(8,128)S(1)} collective-permute-done((f32[512,128]{1,0:T(8,128)S(1)}, f32[512,128]{1,0:T(8,128)S(1)}, u32[]{:S(2)}, u32[]{:S(2)}) %collective-permute-start.16) | collective-permute-done | bytes 262176 | tf_op jit(solution)/shard_map/ppermute | solution.py:403
  102.0 0.8 add_convert_fusion.refs_0_
  102.7 1.6 collective-permute-start.18
  104.4 2.7 %collective-permute-start.20 = (bf16[512,128]{1,0:T(8,128)(2,1)}, bf16[512,128]{1,0:T(8,128)(2,1)}, u32[]{:S(2)}, u32[]{:S(2)}) collective-permute-start(bf16[512,128]{1,0:T(8,128)(2,1)} %add_convert_fusion.refs_0_), channel_id=1, source_target_pairs={{0,72},{8,0},{64,8},{72,64},{1,73},{9,1},{65,9},{73,65},{2,74},{10... | collective-permute-start | bytes 393224 | tf_op jit(solution)/shard_map/ppermute | solution.py:399
  107.1 1.8 collective-permute-start.12
  108.9 4.0 %collective-permute-done.18.refs_1_ = bf16[512,128]{1,0:T(8,128)(2,1)} collective-permute-done((bf16[512,128]{1,0:T(8,128)(2,1)}, bf16[512,128]{1,0:T(8,128)(2,1)}, u32[]{:S(2)}, u32[]{:S(2)}) %collective-permute-start.18) | collective-permute-done | bytes 131104 | tf_op jit(solution)/shard_map/ppermute | solution.py:399
  112.9 1.3 collective-permute-start.14
  114.3 1.3 copy-done.1
  115.6 15.3 %attend.1 = bf16[8,272,128]{2,1,0:T(8,128)(2,1)} custom-call(s32[1]{0:T(128)} %bitcast.6.place_ref, s32[16]{0:T(128)} %slot_ref.1, s32[16,8,128]{2,1,0:T(8,128)} %mask_ref.1, bf16[512,128]{1,0:T(8,128)(2,1)} %add_convert_fusion.refs_0_, bf16[512,128]{1,0:T(8,128)(2,1)} %collective-permute-done.18.refs_1_, bf16[512,128]{1,0:T(8,128)(2,1)} %collective-permute-done.19.refs_2_, ...), custom_call_target="tpu_custom_call" | custom-call | flops 4294967296 | bytes 4194304 | tf_op jit(solution)/shard_map/attend/pallas_call | solution.py:134
  131.7 0.7 copy-done.21
  132.4 2.6 %settle.1.refs_0_ = bf16[640,1024]{1,0:T(8,128)(2,1)} custom-call(s32[4]{0:T(128)} %pad_add_fusion.place_ref, bf16[80,1024]{1,0:T(8,128)(2,1)} %get-tuple-element.63.refs_0_, bf16[80,1024]{1,0:T(8,128)(2,1)} %copy-done.9, bf16[80,1024]{1,0:T(8,128)(2,1)} %copy-done.10, bf16[80,1024]{1,0:T(8,128)(2,1)} %copy-done.8, bf16[80,1024]{1,0:T(8,128)(2,1)} %copy-done.16, ...), custom_call_target="tpu_custom_call" | custom-call | tf_op jit(solution)/shard_map/settle/pallas_call | solution.py:274
  135.0 14.6 %all_to_all.20.part_ref = bf16[8,272,128]{2,1,0:T(8,128)(2,1)} all-to-all(bf16[8,272,128]{2,1,0:T(8,128)(2,1)S(1)} %copy-done.5), channel_id=1, replica_groups=mesh['tm'=2,'y'=4,'zl'=2,'x'=4,'c'=2] {'tm','zl','c'}, dimensions={0} | all-to-all | bytes 1114112 | tf_op jit(solution)/shard_map/all_to_all | solution.py:411
  149.6 2.1 %merge.1.refs_0_ = bf16[256,256]{1,0:T(8,128)(2,1)} custom-call(s32[1]{0:T(128)} %bitcast.2.core_ref, bf16[8,272,128]{2,1,0:T(8,128)(2,1)} %all_to_all.20.part_ref), custom_call_target="tpu_custom_call" | custom-call | tf_op jit(solution)/shard_map/merge/pallas_call | solution.py:171
  151.7 2.0 %collective-permute-start.22 = (bf16[256,256]{1,0:T(8,128)(2,1)}, bf16[256,256]{1,0:T(8,128)(2,1)S(1)}, u32[]{:S(2)}, u32[]{:S(2)}) collective-permute-start(bf16[256,256]{1,0:T(8,128)(2,1)} %merge.1.refs_0_), channel_id=1, source_target_pairs={{0,32},{16,48},{32,0},{48,16},{1,33},{17,49},{33,1},{49,17},{2,34}... | collective-permute-start | bytes 393224 | tf_op jit(solution)/shard_map/ppermute | solution.py:403
  153.7 2.3 %collective-permute-start.23 = (bf16[256,256]{1,0:T(8,128)(2,1)}, bf16[256,256]{1,0:T(8,128)(2,1)S(1)}, u32[]{:S(2)}, u32[]{:S(2)}) collective-permute-start(bf16[256,256]{1,0:T(8,128)(2,1)} %merge.1.refs_0_), channel_id=1, source_target_pairs={{0,48},{16,0},{32,16},{48,32},{1,49},{17,1},{33,17},{49,33},{2,50}... | collective-permute-start | bytes 393224 | tf_op jit(solution)/shard_map/ppermute | solution.py:403
  156.0 1.1 copy-done.2
  157.1 3.4 %weave_out.1.refs_4_ = bf16[1280,1024]{1,0:T(8,128)(2,1)} custom-call(s32[4]{0:T(128)} %pad_add_fusion.place_ref, bf16[640,1024]{1,0:T(8,128)(2,1)} %settle.1.refs_0_, bf16[640,1024]{1,0:T(8,128)(2,1)} %copy-done.2), custom_call_target="tpu_custom_call" | custom-call | tf_op jit(solution)/shard_map/weave_out/pallas_call | solution.py:366
  160.5 0.8 collective-permute-done.21.refs_1_
  162.0 0.7 copy-done.24
  162.6 3.8 %project.1 = bf16[16,16,1280]{2,1,0:T(8,128)(2,1)} custom-call(s32[4]{0:T(128)} %pad_add_fusion.place_ref, bf16[256,256]{1,0:T(8,128)(2,1)} %merge.1.refs_0_, bf16[256,256]{1,0:T(8,128)(2,1)} %copy-done.22, bf16[256,256]{1,0:T(8,128)(2,1)} %copy-done.23, bf16[256,256]{1,0:T(8,128)(2,1)} %copy-done.24, bf16[1280,1024]{1,0:T(8,128)(2,1)} %weave_out.1.refs_4_), custom_call_target="tpu_custom_call" | custom-call | tf_op jit(solution)/shard_map/project/pallas_call | solution.py:195
  166.4 19.6 %all_to_all.21.part_ref = bf16[16,16,1280]{2,1,0:T(8,128)(2,1)} all-to-all(bf16[16,16,1280]{2,1,0:T(8,128)(2,1)} %project.1), channel_id=1, replica_groups=mesh['tm'=2,'y'=4,'zl'=2,'x'=4,'c'=2] {'y','x'}, dimensions={0} | all-to-all | bytes 1310720 | tf_op jit(solution)/shard_map/all_to_all | solution.py:411
  186.0 1.8 finish.1
  (76 shorter events, 3.6 us)
Async XLA Ops:
  2.1 7.6 %copy-start.3 = (bf16[80,4096]{1,0:T(8,128)(2,1)S(1)}, bf16[80,4096]{1,0:T(8,128)(2,1)}, u32[]{:S(2)}) copy-start(bf16[80,4096]{1,0:T(8,128)(2,1)} %near_ref.1) | copy-start | bytes 1966084
  2.1 49.8 %all-to-all-start = ((bf16[32,16,1280]{2,1,0:T(8,128)(2,1)}), bf16[32,16,1280]{2,1,0:T(8,128)(2,1)S(1)}, u32[]{:S(2)}, u32[]{:S(2)}) async-start(bf16[32,16,1280]{2,1,0:T(8,128)(2,1)} %pack_tokens.1), calls=%async_computation | async-start | bytes 2621440 | tf_op jit(solution)/shard_map/all_to_all | solution.py:411
  9.7 2.2 %collective-permute-start = (bf16[80,4096]{1,0:T(8,128)(2,1)S(1)}, bf16[80,4096]{1,0:T(8,128)(2,1)S(1)}, u32[]{:S(2)}, u32[]{:S(2)}) collective-permute-start(bf16[80,4096]{1,0:T(8,128)(2,1)S(1)} %copy-done.3), channel_id=1, source_target_pairs={{0,1},{1,0},{2,3},{3,2},{4,5},{5,4},{6,7},{7,6},{8,9},{9,8},{10,11... | collective-permute-start | bytes 1966088 | tf_op jit(solution)/shard_map/ppermute | solution.py:407
  11.8 0.9 copy-start.4
  15.0 16.3 %collective-permute-start.1 = (bf16[2,80,512]{2,1,0:T(8,128)(2,1)}, bf16[2,80,512]{2,1,0:T(8,128)(2,1)S(1)}, u32[]{:S(2)}, u32[]{:S(2)}) collective-permute-start(bf16[2,80,512]{2,1,0:T(8,128)(2,1)} %get-tuple-element.39), channel_id=1, source_target_pairs={{0,2},{2,4},{4,6},{6,0},{1,3},{3,5},{5,7},{7,1},{8,10},{10,12},{12... | collective-permute-start | bytes 491528 | tf_op jit(solution)/shard_map/ppermute | solution.py:403
  16.8 18.5 %collective-permute-start.2 = (bf16[2,80,512]{2,1,0:T(8,128)(2,1)}, bf16[2,80,512]{2,1,0:T(8,128)(2,1)S(1)}, u32[]{:S(2)}, u32[]{:S(2)}) collective-permute-start(bf16[2,80,512]{2,1,0:T(8,128)(2,1)} %get-tuple-element.40), channel_id=1, source_target_pairs={{0,4},{2,6},{4,0},{6,2},{1,5},{3,7},{5,1},{7,3},{8,12},{10,14},{12... | collective-permute-start | bytes 491528 | tf_op jit(solution)/shard_map/ppermute | solution.py:403
  19.5 19.9 %collective-permute-start.3 = (bf16[2,80,512]{2,1,0:T(8,128)(2,1)}, bf16[2,80,512]{2,1,0:T(8,128)(2,1)S(1)}, u32[]{:S(2)}, u32[]{:S(2)}) collective-permute-start(bf16[2,80,512]{2,1,0:T(8,128)(2,1)} %get-tuple-element.41), channel_id=1, source_target_pairs={{0,6},{2,0},{4,2},{6,4},{1,7},{3,1},{5,3},{7,5},{8,14},{10,8},{12,... | collective-permute-start | bytes 491528 | tf_op jit(solution)/shard_map/ppermute | solution.py:403
  20.9 20.9 %collective-permute-start.4 = (bf16[2,80,512]{2,1,0:T(8,128)(2,1)}, bf16[2,80,512]{2,1,0:T(8,128)(2,1)S(1)}, u32[]{:S(2)}, u32[]{:S(2)}) collective-permute-start(bf16[2,80,512]{2,1,0:T(8,128)(2,1)} %get-tuple-element.38.refs_0_), channel_id=1, source_target_pairs={{0,8},{8,64},{64,72},{72,0},{1,9},{9,65},{65,73},{73,1},{2,10},{10... | collective-permute-start | bytes 491528 | tf_op jit(solution)/shard_map/ppermute | solution.py:399
  31.3 16.4 %copy-start.11 = (bf16[2,80,512]{2,1,0:T(8,128)(2,1)}, bf16[2,80,512]{2,1,0:T(8,128)(2,1)S(1)}, u32[]{:S(2)}) copy-start(bf16[2,80,512]{2,1,0:T(8,128)(2,1)S(1)} %collective-permute-done.1.refs_1_) | copy-start | bytes 491524
  31.3 12.6 %collective-permute-start.5 = (bf16[2,80,512]{2,1,0:T(8,128)(2,1)S(1)}, bf16[2,80,512]{2,1,0:T(8,128)(2,1)S(1)}, u32[]{:S(2)}, u32[]{:S(2)}) collective-permute-start(bf16[2,80,512]{2,1,0:T(8,128)(2,1)S(1)} %collective-permute-done.1.refs_1_), channel_id=1, source_target_pairs={{0,8},{8,64},{64,72},{72,0},{1,9},{9,65},{65,73},{73,1},{2,10},{10... | collective-permute-start | bytes 491528 | tf_op jit(solution)/shard_map/ppermute | solution.py:399
  35.3 12.4 %copy-start.12 = (bf16[2,80,512]{2,1,0:T(8,128)(2,1)}, bf16[2,80,512]{2,1,0:T(8,128)(2,1)S(1)}, u32[]{:S(2)}) copy-start(bf16[2,80,512]{2,1,0:T(8,128)(2,1)S(1)} %collective-permute-done.2.refs_2_) | copy-start | bytes 491524
  35.3 12.4 %collective-permute-start.6 = (bf16[2,80,512]{2,1,0:T(8,128)(2,1)S(1)}, bf16[2,80,512]{2,1,0:T(8,128)(2,1)S(1)}, u32[]{:S(2)}, u32[]{:S(2)}) collective-permute-start(bf16[2,80,512]{2,1,0:T(8,128)(2,1)S(1)} %collective-permute-done.2.refs_2_), channel_id=1, source_target_pairs={{0,72},{8,0},{64,8},{72,64},{1,73},{9,1},{65,9},{73,65},{2,74},{10... | collective-permute-start | bytes 491528 | tf_op jit(solution)/shard_map/ppermute | solution.py:399
  39.4 8.3 %copy-start.13 = (bf16[2,80,512]{2,1,0:T(8,128)(2,1)}, bf16[2,80,512]{2,1,0:T(8,128)(2,1)S(1)}, u32[]{:S(2)}) copy-start(bf16[2,80,512]{2,1,0:T(8,128)(2,1)S(1)} %collective-permute-done.3.refs_3_) | copy-start | bytes 491524
  39.4 8.4 %collective-permute-start.7 = (bf16[2,80,512]{2,1,0:T(8,128)(2,1)S(1)}, bf16[2,80,512]{2,1,0:T(8,128)(2,1)S(1)}, u32[]{:S(2)}, u32[]{:S(2)}) collective-permute-start(bf16[2,80,512]{2,1,0:T(8,128)(2,1)S(1)} %collective-permute-done.3.refs_3_), channel_id=1, source_target_pairs={{0,72},{8,0},{64,8},{72,64},{1,73},{9,1},{65,9},{73,65},{2,74},{10... | collective-permute-start | bytes 491528 | tf_op jit(solution)/shard_map/ppermute | solution.py:399
  41.8 14.7 %collective-permute-start.10 = (bf16[80,1024]{1,0:T(8,128)(2,1)}, bf16[80,1024]{1,0:T(8,128)(2,1)S(1)}, u32[]{:S(2)}, u32[]{:S(2)}) collective-permute-start(bf16[80,1024]{1,0:T(8,128)(2,1)} %get-tuple-element.52), channel_id=1, source_target_pairs={{0,6},{2,0},{4,2},{6,4},{1,7},{3,1},{5,3},{7,5},{8,14},{10,8},{12,... | collective-permute-start | bytes 491528 | tf_op jit(solution)/shard_map/ppermute | solution.py:403
  41.9 5.8 %copy-start.14 = (bf16[2,80,512]{2,1,0:T(8,128)(2,1)}, bf16[2,80,512]{2,1,0:T(8,128)(2,1)S(1)}, u32[]{:S(2)}) copy-start(bf16[2,80,512]{2,1,0:T(8,128)(2,1)S(1)} %collective-permute-done.4.refs_4_) | copy-start | bytes 491524
  41.9 14.7 %collective-permute-start.8 = (bf16[80,1024]{1,0:T(8,128)(2,1)}, bf16[80,1024]{1,0:T(8,128)(2,1)S(1)}, u32[]{:S(2)}, u32[]{:S(2)}) collective-permute-start(bf16[80,1024]{1,0:T(8,128)(2,1)} %get-tuple-element.50), channel_id=1, source_target_pairs={{0,2},{2,4},{4,6},{6,0},{1,3},{3,5},{5,7},{7,1},{8,10},{10,12},{12... | collective-permute-start | bytes 491528 | tf_op jit(solution)/shard_map/ppermute | solution.py:403
  43.9 3.8 %copy-start.15 = (bf16[2,80,512]{2,1,0:T(8,128)(2,1)}, bf16[2,80,512]{2,1,0:T(8,128)(2,1)S(1)}, u32[]{:S(2)}) copy-start(bf16[2,80,512]{2,1,0:T(8,128)(2,1)S(1)} %collective-permute-done.5.refs_5_) | copy-start | bytes 491524
  43.9 12.7 %collective-permute-start.9 = (bf16[80,1024]{1,0:T(8,128)(2,1)}, bf16[80,1024]{1,0:T(8,128)(2,1)S(1)}, u32[]{:S(2)}, u32[]{:S(2)}) collective-permute-start(bf16[80,1024]{1,0:T(8,128)(2,1)} %get-tuple-element.51), channel_id=1, source_target_pairs={{0,4},{2,6},{4,0},{6,2},{1,5},{3,7},{5,1},{7,3},{8,12},{10,14},{12... | collective-permute-start | bytes 491528 | tf_op jit(solution)/shard_map/ppermute | solution.py:403
  51.9 1.1 copy-start
  56.5 56.3 %copy-start.8 = (bf16[80,1024]{1,0:T(8,128)(2,1)}, bf16[80,1024]{1,0:T(8,128)(2,1)S(1)}, u32[]{:S(2)}) copy-start(bf16[80,1024]{1,0:T(8,128)(2,1)S(1)} %collective-permute-done.10.refs_3_) | copy-start | bytes 491524
  56.5 50.5 %copy-start.9 = (bf16[80,1024]{1,0:T(8,128)(2,1)}, bf16[80,1024]{1,0:T(8,128)(2,1)S(1)}, u32[]{:S(2)}) copy-start(bf16[80,1024]{1,0:T(8,128)(2,1)S(1)} %collective-permute-done.8.refs_1_) | copy-start | bytes 491524
  56.5 56.3 %copy-start.10 = (bf16[80,1024]{1,0:T(8,128)(2,1)}, bf16[80,1024]{1,0:T(8,128)(2,1)S(1)}, u32[]{:S(2)}) copy-start(bf16[80,1024]{1,0:T(8,128)(2,1)S(1)} %collective-permute-done.9.refs_2_) | copy-start | bytes 491524
  56.6 9.2 %copy-start.26 = (f32[512,128]{1,0:T(8,128)S(1)}, f32[512,128]{1,0:T(8,128)}, u32[]{:S(2)}) copy-start(f32[512,128]{1,0:T(8,128)} %get-tuple-element.59) | copy-start | bytes 786436
  56.6 11.9 %copy-start.25 = (f32[512,128]{1,0:T(8,128)S(1)}, f32[512,128]{1,0:T(8,128)}, u32[]{:S(2)}) copy-start(f32[512,128]{1,0:T(8,128)} %get-tuple-element.60) | copy-start | bytes 786436
  56.6 45.4 %copy-start.6 = (f32[512,128]{1,0:T(8,128)S(1)}, f32[512,128]{1,0:T(8,128)}, u32[]{:S(2)}) copy-start(f32[512,128]{1,0:T(8,128)} %get-tuple-element.57) | copy-start | bytes 786436
  56.6 50.5 %copy-start.7 = (bf16[80,1024]{1,0:T(8,128)(2,1)S(1)}, bf16[80,1024]{1,0:T(8,128)(2,1)}, u32[]{:S(2)}) copy-start(bf16[80,1024]{1,0:T(8,128)(2,1)} %get-tuple-element.63.refs_0_) | copy-start | bytes 491524
  56.6 57.7 %all-to-all-start.1 = ((bf16[32,256,128]{2,1,0:T(8,128)(2,1)}), bf16[32,256,128]{2,1,0:T(8,128)(2,1)S(1)}, u32[]{:S(2)}, u32[]{:S(2)}) async-start(bf16[32,256,128]{2,1,0:T(8,128)(2,1)} %pack_cache.1), calls=%async_computation.1 | async-start | bytes 4194304 | tf_op jit(solution)/shard_map/all_to_all | solution.py:411
  63.9 32.5 %collective-permute-start.15 = (f32[512,128]{1,0:T(8,128)}, f32[512,128]{1,0:T(8,128)S(1)}, u32[]{:S(2)}, u32[]{:S(2)}) collective-permute-start(f32[512,128]{1,0:T(8,128)} %get-tuple-element.58), channel_id=1, source_target_pairs={{0,16},{16,32},{32,48},{48,0},{1,17},{17,33},{33,49},{49,1},{2,18}... | collective-permute-start | bytes 786440 | tf_op jit(solution)/shard_map/ppermute | solution.py:403
  65.8 36.2 %collective-permute-start.16 = (f32[512,128]{1,0:T(8,128)S(1)}, f32[512,128]{1,0:T(8,128)S(1)}, u32[]{:S(2)}, u32[]{:S(2)}) collective-permute-start(f32[512,128]{1,0:T(8,128)S(1)} %copy-done.26), channel_id=1, source_target_pairs={{0,32},{16,48},{32,0},{48,16},{1,33},{17,49},{33,1},{49,17},{2,34}... | collective-permute-start | bytes 786440 | tf_op jit(solution)/shard_map/ppermute | solution.py:403
  68.5 33.5 %collective-permute-start.17 = (f32[512,128]{1,0:T(8,128)S(1)}, f32[512,128]{1,0:T(8,128)S(1)}, u32[]{:S(2)}, u32[]{:S(2)}) collective-permute-start(f32[512,128]{1,0:T(8,128)S(1)} %copy-done.25), channel_id=1, source_target_pairs={{0,48},{16,0},{32,16},{48,32},{1,49},{17,1},{33,17},{49,33},{2,50}... | collective-permute-start | bytes 786440 | tf_op jit(solution)/shard_map/ppermute | solution.py:403
  102.7 10.1 %collective-permute-start.18 = (bf16[512,128]{1,0:T(8,128)(2,1)}, bf16[512,128]{1,0:T(8,128)(2,1)}, u32[]{:S(2)}, u32[]{:S(2)}) collective-permute-start(bf16[512,128]{1,0:T(8,128)(2,1)} %add_convert_fusion.refs_0_), channel_id=1, source_target_pairs={{0,8},{8,64},{64,72},{72,0},{1,9},{9,65},{65,73},{73,1},{2,10},{10... | collective-permute-start | bytes 393224 | tf_op jit(solution)/shard_map/ppermute | solution.py:399
  104.4 8.5 %collective-permute-start.19 = (bf16[512,128]{1,0:T(8,128)(2,1)}, bf16[512,128]{1,0:T(8,128)(2,1)}, u32[]{:S(2)}, u32[]{:S(2)}) collective-permute-start(bf16[512,128]{1,0:T(8,128)(2,1)} %add_convert_fusion.refs_0_), channel_id=1, source_target_pairs={{0,64},{8,72},{64,0},{72,8},{1,65},{9,73},{65,1},{73,9},{2,66},{10... | collective-permute-start | bytes 393224 | tf_op jit(solution)/shard_map/ppermute | solution.py:399
  104.4 9.9 %collective-permute-start.20 = (bf16[512,128]{1,0:T(8,128)(2,1)}, bf16[512,128]{1,0:T(8,128)(2,1)}, u32[]{:S(2)}, u32[]{:S(2)}) collective-permute-start(bf16[512,128]{1,0:T(8,128)(2,1)} %add_convert_fusion.refs_0_), channel_id=1, source_target_pairs={{0,72},{8,0},{64,8},{72,64},{1,73},{9,1},{65,9},{73,65},{2,74},{10... | collective-permute-start | bytes 393224 | tf_op jit(solution)/shard_map/ppermute | solution.py:399
  107.0 23.9 %collective-permute-start.11 = (bf16[80,1024]{1,0:T(8,128)(2,1)S(1)}, bf16[80,1024]{1,0:T(8,128)(2,1)S(1)}, u32[]{:S(2)}, u32[]{:S(2)}) collective-permute-start(bf16[80,1024]{1,0:T(8,128)(2,1)S(1)} %copy-done.7), channel_id=1, source_target_pairs={{0,8},{8,64},{64,72},{72,0},{1,9},{9,65},{65,73},{73,1},{2,10},{10... | collective-permute-start | bytes 491528 | tf_op jit(solution)/shard_map/ppermute | solution.py:399
  107.1 23.9 %collective-permute-start.12 = (bf16[80,1024]{1,0:T(8,128)(2,1)S(1)}, bf16[80,1024]{1,0:T(8,128)(2,1)S(1)}, u32[]{:S(2)}, u32[]{:S(2)}) collective-permute-start(bf16[80,1024]{1,0:T(8,128)(2,1)S(1)} %collective-permute-done.8.refs_1_), channel_id=1, source_target_pairs={{0,8},{8,64},{64,72},{72,0},{1,9},{9,65},{65,73},{73,1},{2,10},{10... | collective-permute-start | bytes 491528 | tf_op jit(solution)/shard_map/ppermute | solution.py:399
  112.8 18.1 %collective-permute-start.13 = (bf16[80,1024]{1,0:T(8,128)(2,1)S(1)}, bf16[80,1024]{1,0:T(8,128)(2,1)S(1)}, u32[]{:S(2)}, u32[]{:S(2)}) collective-permute-start(bf16[80,1024]{1,0:T(8,128)(2,1)S(1)} %collective-permute-done.9.refs_2_), channel_id=1, source_target_pairs={{0,72},{8,0},{64,8},{72,64},{1,73},{9,1},{65,9},{73,65},{2,74},{10... | collective-permute-start | bytes 491528 | tf_op jit(solution)/shard_map/ppermute | solution.py:399
  112.9 18.1 %collective-permute-start.14 = (bf16[80,1024]{1,0:T(8,128)(2,1)S(1)}, bf16[80,1024]{1,0:T(8,128)(2,1)S(1)}, u32[]{:S(2)}, u32[]{:S(2)}) collective-permute-start(bf16[80,1024]{1,0:T(8,128)(2,1)S(1)} %collective-permute-done.10.refs_3_), channel_id=1, source_target_pairs={{0,72},{8,0},{64,8},{72,64},{1,73},{9,1},{65,9},{73,65},{2,74},{10... | collective-permute-start | bytes 491528 | tf_op jit(solution)/shard_map/ppermute | solution.py:399
  114.3 1.3 copy-start.1
  130.9 4.0 %copy-start.5 = (bf16[8,272,128]{2,1,0:T(8,128)(2,1)S(1)}, bf16[8,272,128]{2,1,0:T(8,128)(2,1)}, u32[]{:S(2)}) copy-start(bf16[8,272,128]{2,1,0:T(8,128)(2,1)} %attend.1) | copy-start | bytes 1671172
  131.0 0.7 copy-start.17
  131.0 0.7 copy-start.19
  135.0 21.1 %collective-permute-start.24 = (bf16[640,1024]{1,0:T(8,128)(2,1)}, bf16[640,1024]{1,0:T(8,128)(2,1)S(1)}, u32[]{:S(2)}, u32[]{:S(2)}) collective-permute-start(bf16[640,1024]{1,0:T(8,128)(2,1)} %settle.1.refs_0_), channel_id=1, source_target_pairs={{0,1},{1,0},{2,3},{3,2},{4,5},{5,4},{6,7},{7,6},{8,9},{9,8},{10,11... | collective-permute-start | bytes 3932168 | tf_op jit(solution)/shard_map/ppermute | solution.py:407
  151.7 9.6 %collective-permute-start.21 = (bf16[256,256]{1,0:T(8,128)(2,1)}, bf16[256,256]{1,0:T(8,128)(2,1)S(1)}, u32[]{:S(2)}, u32[]{:S(2)}) collective-permute-start(bf16[256,256]{1,0:T(8,128)(2,1)} %merge.1.refs_0_), channel_id=1, source_target_pairs={{0,16},{16,32},{32,48},{48,0},{1,17},{17,33},{33,49},{49,1},{2,18}... | collective-permute-start | bytes 393224 | tf_op jit(solution)/shard_map/ppermute | solution.py:403
  151.7 9.6 %collective-permute-start.22 = (bf16[256,256]{1,0:T(8,128)(2,1)}, bf16[256,256]{1,0:T(8,128)(2,1)S(1)}, u32[]{:S(2)}, u32[]{:S(2)}) collective-permute-start(bf16[256,256]{1,0:T(8,128)(2,1)} %merge.1.refs_0_), channel_id=1, source_target_pairs={{0,32},{16,48},{32,0},{48,16},{1,33},{17,49},{33,1},{49,17},{2,34}... | collective-permute-start | bytes 393224 | tf_op jit(solution)/shard_map/ppermute | solution.py:403
  153.7 8.2 %collective-permute-start.23 = (bf16[256,256]{1,0:T(8,128)(2,1)}, bf16[256,256]{1,0:T(8,128)(2,1)S(1)}, u32[]{:S(2)}, u32[]{:S(2)}) collective-permute-start(bf16[256,256]{1,0:T(8,128)(2,1)} %merge.1.refs_0_), channel_id=1, source_target_pairs={{0,48},{16,0},{32,16},{48,32},{1,49},{17,1},{33,17},{49,33},{2,50}... | collective-permute-start | bytes 393224 | tf_op jit(solution)/shard_map/ppermute | solution.py:403
  156.0 1.1 copy-start.2
  161.3 0.7 copy-start.23
  (6 other events, 4.0 us)

commit v3 on v2

--- a/solution.py
+++ b/solution.py
@@ -403,6 +403,12 @@
     return lax.ppermute(value, axis, [(i, (i + shift) % 4) for i in range(4)])
 
 
+def far_first(parts, axis):
+    far = ring_shift(parts[2], axis, 2)
+    near = [ring_shift(parts[s], axis, s) for s in (1, 3)]
+    return [parts[0], near[0], far, near[1]]
+
+
 def core_swap(value):
     return lax.ppermute(value, "c", [(0, 1), (1, 0)])
 
@@ -431,7 +437,7 @@
 
     partial = query_parts(token_rows.reshape(-1, token_rows.shape[2]), weights)
     partial, cache, got_out = lax.optimization_barrier((partial, cache, got_out))
-    partial = [partial[0]] + [ring_shift(partial[s], "y", s) for s in (1, 2, 3)]
+    partial = far_first(partial, "y")
     arrived = exchange(cache, PLANE)
     got_out = list(got_out)
     got_out += [z_shift(got_out[s], 1) for s in (0, 1)]

time: 189 us -> 189 us (level)
  no operation moved by 1% of the time
where the time goes in v3:
time: 189 us; the launch traced here: 188 us
  starting transfers between devices  49.7 us (26%)
  waiting for transfers between devices  49.3 us (26%)
  Pallas kernels  45 us (24%)
  blocking collectives  34.2 us (18%)
  local copies, waits for them, and re-layouts  7.93 us (4%)
    ppermute x12, waiting for transfers between devices, ring_shift(): return lax.ppermute(value, axis, [(i, (i + shift) % 4) for i in range(4)])  44 us
    all_to_all x2, blocking collectives, exchange(): return lax.all_to_all(table, axes, split_axis=0, concat_axis=0, tiled=True)  34.2 us
    ppermute x12, starting transfers between devices, ring_shift(): return lax.ppermute(value, axis, [(i, (i + shift) % 4) for i in range(4)])  18.8 us
    ppermute x11, starting transfers between devices, z_shift(): lax.ppermute(value, ('tm', 'zl'), [(i, (i + shift) % 4) for i in range(4)])  15.7 us
    pallas_call x1, Pallas kernels, attend(): pl.pallas_call(attention_kernel, out_shape=jax.ShapeDtypeStruct((8, 272,...  15.3 us
    all_to_all x2, starting transfers between devices, exchange(): return lax.all_to_all(table, axes, split_axis=0, concat_axis=0, tiled=True)  14.8 us
    unnamed x54, local copies, waits for them, and re-layouts  7.93 us
    ppermute x11, waiting for transfers between devices, z_shift(): lax.ppermute(value, ('tm', 'zl'), [(i, (i + shift) % 4) for i in range(4)])  4.13 us
  transfers between devices with their start and end apart: 27, of which 9 were waited for; matrix products, arithmetic and copies ran while one was open for 1% of the time, Pallas kernels for 18%

profile of v3, /device:TPU:0, one launch (start us, length us, event | category | flops | bytes accessed | tf_op | source)
XLA Modules:
  0.0 187.8 jit_solution(18423350564387232904)
XLA Ops:
  0.0 2.1 %pack_tokens.1 = bf16[32,16,1280]{2,1,0:T(8,128)(2,1)} custom-call(bf16[16,5120]{1,0:T(8,128)(2,1)} %token_ref.1), custom_call_target="tpu_custom_call" | custom-call | tf_op jit(solution)/shard_map/pack_tokens/pallas_call | solution.py:252
  2.1 7.6 %all-to-all-start = ((bf16[32,16,1280]{2,1,0:T(8,128)(2,1)}), bf16[32,16,1280]{2,1,0:T(8,128)(2,1)S(1)}, u32[]{:S(2)}, u32[]{:S(2)}) async-start(bf16[32,16,1280]{2,1,0:T(8,128)(2,1)} %pack_tokens.1), calls=%async_computation | async-start | bytes 2621440 | tf_op jit(solution)/shard_map/all_to_all | solution.py:417
  10.0 0.7 pad_add_fusion.place_ref
  10.7 1.2 collective-permute-done.far_ref
  11.9 0.9 copy-done.4
  12.7 2.3 %pack_query.1 = (bf16[2,80,512]{2,1,0:T(8,128)(2,1)}, bf16[2,80,512]{2,1,0:T(8,128)(2,1)}, bf16[2,80,512]{2,1,0:T(8,128)(2,1)}, bf16[2,80,512]{2,1,0:T(8,128)(2,1)}) custom-call(s32[4]{0:T(128)} %pad_add_fusion.place_ref, bf16[80,4096]{1,0:T(8,128)(2,1)} %near_ref.1, bf16[80,4096]{1,0:T(8,128)(2,1)} %copy-done.4), custom_call_target="tpu_custom_call" | custom-call | tf_op jit(solution)/shard_map/pack_query/pallas_call | solution.py:217
  15.0 1.8 collective-permute-start.1
  16.8 2.7 %collective-permute-start.2 = (bf16[2,80,512]{2,1,0:T(8,128)(2,1)}, bf16[2,80,512]{2,1,0:T(8,128)(2,1)S(1)}, u32[]{:S(2)}, u32[]{:S(2)}) collective-permute-start(bf16[2,80,512]{2,1,0:T(8,128)(2,1)} %get-tuple-element.40), channel_id=1, source_target_pairs={{0,4},{2,6},{4,0},{6,2},{1,5},{3,7},{5,1},{7,3},{8,12},{10,14},{12... | collective-permute-start | bytes 491528 | tf_op jit(solution)/shard_map/ppermute | solution.py:403
  19.5 1.5 collective-permute-start.3
  20.9 1.9 %collective-permute-start.4 = (bf16[2,80,512]{2,1,0:T(8,128)(2,1)}, bf16[2,80,512]{2,1,0:T(8,128)(2,1)S(1)}, u32[]{:S(2)}, u32[]{:S(2)}) collective-permute-start(bf16[2,80,512]{2,1,0:T(8,128)(2,1)} %get-tuple-element.38.refs_0_), channel_id=1, source_target_pairs={{0,8},{8,64},{64,72},{72,0},{1,9},{9,65},{65,73},{73,1},{2,10},{10... | collective-permute-start | bytes 491528 | tf_op jit(solution)/shard_map/ppermute | solution.py:399
  22.8 8.5 %collective-permute-done.1.refs_1_ = bf16[2,80,512]{2,1,0:T(8,128)(2,1)S(1)} collective-permute-done((bf16[2,80,512]{2,1,0:T(8,128)(2,1)}, bf16[2,80,512]{2,1,0:T(8,128)(2,1)S(1)}, u32[]{:S(2)}, u32[]{:S(2)}) %collective-permute-start.1) | collective-permute-done | bytes 163872 | tf_op jit(solution)/shard_map/ppermute | solution.py:403
  31.3 1.9 %collective-permute-start.5 = (bf16[2,80,512]{2,1,0:T(8,128)(2,1)S(1)}, bf16[2,80,512]{2,1,0:T(8,128)(2,1)S(1)}, u32[]{:S(2)}, u32[]{:S(2)}) collective-permute-start(bf16[2,80,512]{2,1,0:T(8,128)(2,1)S(1)} %collective-permute-done.1.refs_1_), channel_id=1, source_target_pairs={{0,8},{8,64},{64,72},{72,0},{1,9},{9,65},{65,73},{73,1},{2,10},{10... | collective-permute-start | bytes 491528 | tf_op jit(solution)/shard_map/ppermute | solution.py:399
  33.2 2.1 %collective-permute-done.2.refs_2_ = bf16[2,80,512]{2,1,0:T(8,128)(2,1)S(1)} collective-permute-done((bf16[2,80,512]{2,1,0:T(8,128)(2,1)}, bf16[2,80,512]{2,1,0:T(8,128)(2,1)S(1)}, u32[]{:S(2)}, u32[]{:S(2)}) %collective-permute-start.2) | collective-permute-done | bytes 163872 | tf_op jit(solution)/shard_map/ppermute | solution.py:403
  35.3 4.0 %collective-permute-start.6 = (bf16[2,80,512]{2,1,0:T(8,128)(2,1)S(1)}, bf16[2,80,512]{2,1,0:T(8,128)(2,1)S(1)}, u32[]{:S(2)}, u32[]{:S(2)}) collective-permute-start(bf16[2,80,512]{2,1,0:T(8,128)(2,1)S(1)} %collective-permute-done.2.refs_2_), channel_id=1, source_target_pairs={{0,72},{8,0},{64,8},{72,64},{1,73},{9,1},{65,9},{73,65},{2,74},{10... | collective-permute-start | bytes 491528 | tf_op jit(solution)/shard_map/ppermute | solution.py:399
  39.8 2.1 %pack_out.1 = (bf16[80,1024]{1,0:T(8,128)(2,1)}, bf16[80,1024]{1,0:T(8,128)(2,1)}, bf16[80,1024]{1,0:T(8,128)(2,1)}, bf16[80,1024]{1,0:T(8,128)(2,1)}) custom-call(s32[4]{0:T(128)} %pad_add_fusion.place_ref, bf16[80,4096]{1,0:T(8,128)(2,1)} %bitcast.8), custom_call_target="tpu_custom_call" | custom-call | tf_op jit(solution)/shard_map/pack_out/pallas_call | solution.py:315
  41.9 2.0 %collective-permute-start.8 = (bf16[80,1024]{1,0:T(8,128)(2,1)}, bf16[80,1024]{1,0:T(8,128)(2,1)S(1)}, u32[]{:S(2)}, u32[]{:S(2)}) collective-permute-start(bf16[80,1024]{1,0:T(8,128)(2,1)} %get-tuple-element.50), channel_id=1, source_target_pairs={{0,2},{2,4},{4,6},{6,0},{1,3},{3,5},{5,7},{7,1},{8,10},{10,12},{12... | collective-permute-start | bytes 491528 | tf_op jit(solution)/shard_map/ppermute | solution.py:403
  44.4 3.2 %pack_cache.1 = bf16[32,256,128]{2,1,0:T(8,128)(2,1)} custom-call(bf16[128,4096]{1,0:T(8,128)(2,1)} %k_ref.1, bf16[128,4096]{1,0:T(8,128)(2,1)} %v_ref.1), custom_call_target="tpu_custom_call" | custom-call | tf_op jit(solution)/shard_map/pack_cache/pallas_call | solution.py:234
  48.4 0.7 copy-done.20
  49.1 2.8 %weave_query.1.w_ref = bf16[1280,512]{1,0:T(8,128)(2,1)} custom-call(s32[4]{0:T(128)} %pad_add_fusion.place_ref, bf16[2,80,512]{2,1,0:T(8,128)(2,1)} %get-tuple-element.38.refs_0_, bf16[2,80,512]{2,1,0:T(8,128)(2,1)} %copy-done.11, bf16[2,80,512]{2,1,0:T(8,128)(2,1)} %copy-done.12, bf16[2,80,512]{2,1,0:T(8,128)(2,1)} %copy-done.13, ...), custom_call_target="tpu_custom_call" | custom-call | tf_op jit(solution)/shard_map/weave_query/pallas_call | solution.py:343
  51.9 1.1 copy-done
  53.0 3.5 %query_parts.1 = (f32[512,128]{1,0:T(8,128)}, f32[512,128]{1,0:T(8,128)}, f32[512,128]{1,0:T(8,128)}, f32[512,128]{1,0:T(8,128)}) custom-call(bf16[512,1280]{1,0:T(8,128)(2,1)} %bitcast.7, bf16[1280,512]{1,0:T(8,128)(2,1)} %weave_query.1.w_ref), custom_call_target="tpu_custom_call" | custom-call | flops 671088640 | bytes 4194304 | tf_op jit(solution)/shard_map/query_parts/pallas_call | solution.py:386
  56.6 7.3 %all-to-all-start.1 = ((bf16[32,256,128]{2,1,0:T(8,128)(2,1)}), bf16[32,256,128]{2,1,0:T(8,128)(2,1)S(1)}, u32[]{:S(2)}, u32[]{:S(2)}) async-start(bf16[32,256,128]{2,1,0:T(8,128)(2,1)} %pack_cache.1), calls=%async_computation.1 | async-start | bytes 4194304 | tf_op jit(solution)/shard_map/all_to_all | solution.py:417
  63.9 1.9 collective-permute-start.15
  65.8 2.7 %collective-permute-start.16 = (f32[512,128]{1,0:T(8,128)S(1)}, f32[512,128]{1,0:T(8,128)S(1)}, u32[]{:S(2)}, u32[]{:S(2)}) collective-permute-start(f32[512,128]{1,0:T(8,128)S(1)} %copy-done.26), channel_id=1, source_target_pairs={{0,32},{16,48},{32,0},{48,16},{1,33},{17,49},{33,1},{49,17},{2,34}... | collective-permute-start | bytes 786440 | tf_op jit(solution)/shard_map/ppermute | solution.py:403
  68.5 1.4 collective-permute-start.17
  69.9 26.5 %collective-permute-done.15 = f32[512,128]{1,0:T(8,128)S(1)} collective-permute-done((f32[512,128]{1,0:T(8,128)}, f32[512,128]{1,0:T(8,128)S(1)}, u32[]{:S(2)}, u32[]{:S(2)}) %collective-permute-start.15) | collective-permute-done | bytes 262176 | tf_op jit(solution)/shard_map/ppermute | solution.py:403
  96.4 5.6 %collective-permute-done.16 = f32[512,128]{1,0:T(8,128)S(1)} collective-permute-done((f32[512,128]{1,0:T(8,128)S(1)}, f32[512,128]{1,0:T(8,128)S(1)}, u32[]{:S(2)}, u32[]{:S(2)}) %collective-permute-start.16) | collective-permute-done | bytes 262176 | tf_op jit(solution)/shard_map/ppermute | solution.py:403
  102.0 0.8 add_convert_fusion.refs_0_
  102.7 1.6 collective-permute-start.18
  104.4 2.7 %collective-permute-start.20 = (bf16[512,128]{1,0:T(8,128)(2,1)}, bf16[512,128]{1,0:T(8,128)(2,1)}, u32[]{:S(2)}, u32[]{:S(2)}) collective-permute-start(bf16[512,128]{1,0:T(8,128)(2,1)} %add_convert_fusion.refs_0_), channel_id=1, source_target_pairs={{0,72},{8,0},{64,8},{72,64},{1,73},{9,1},{65,9},{73,65},{2,74},{10... | collective-permute-start | bytes 393224 | tf_op jit(solution)/shard_map/ppermute | solution.py:399
  107.1 1.8 collective-permute-start.12
  108.9 4.0 %collective-permute-done.18.refs_1_ = bf16[512,128]{1,0:T(8,128)(2,1)} collective-permute-done((bf16[512,128]{1,0:T(8,128)(2,1)}, bf16[512,128]{1,0:T(8,128)(2,1)}, u32[]{:S(2)}, u32[]{:S(2)}) %collective-permute-start.18) | collective-permute-done | bytes 131104 | tf_op jit(solution)/shard_map/ppermute | solution.py:399
  112.9 1.3 collective-permute-start.14
  114.3 1.3 copy-done.1
  115.6 15.3 %attend.1 = bf16[8,272,128]{2,1,0:T(8,128)(2,1)} custom-call(s32[1]{0:T(128)} %bitcast.6.place_ref, s32[16]{0:T(128)} %slot_ref.1, s32[16,8,128]{2,1,0:T(8,128)} %mask_ref.1, bf16[512,128]{1,0:T(8,128)(2,1)} %add_convert_fusion.refs_0_, bf16[512,128]{1,0:T(8,128)(2,1)} %collective-permute-done.18.refs_1_, bf16[512,128]{1,0:T(8,128)(2,1)} %collective-permute-done.19.refs_2_, ...), custom_call_target="tpu_custom_call" | custom-call | flops 4294967296 | bytes 4194304 | tf_op jit(solution)/shard_map/attend/pallas_call | solution.py:134
  131.7 0.7 copy-done.21
  132.4 2.6 %settle.1.refs_0_ = bf16[640,1024]{1,0:T(8,128)(2,1)} custom-call(s32[4]{0:T(128)} %pad_add_fusion.place_ref, bf16[80,1024]{1,0:T(8,128)(2,1)} %get-tuple-element.63.refs_0_, bf16[80,1024]{1,0:T(8,128)(2,1)} %copy-done.9, bf16[80,1024]{1,0:T(8,128)(2,1)} %copy-done.10, bf16[80,1024]{1,0:T(8,128)(2,1)} %copy-done.8, bf16[80,1024]{1,0:T(8,128)(2,1)} %copy-done.16, ...), custom_call_target="tpu_custom_call" | custom-call | tf_op jit(solution)/shard_map/settle/pallas_call | solution.py:274
  135.0 14.6 %all_to_all.20.part_ref = bf16[8,272,128]{2,1,0:T(8,128)(2,1)} all-to-all(bf16[8,272,128]{2,1,0:T(8,128)(2,1)S(1)} %copy-done.5), channel_id=1, replica_groups=mesh['tm'=2,'y'=4,'zl'=2,'x'=4,'c'=2] {'tm','zl','c'}, dimensions={0} | all-to-all | bytes 1114112 | tf_op jit(solution)/shard_map/all_to_all | solution.py:417
  149.6 2.1 %merge.1.refs_0_ = bf16[256,256]{1,0:T(8,128)(2,1)} custom-call(s32[1]{0:T(128)} %bitcast.2.core_ref, bf16[8,272,128]{2,1,0:T(8,128)(2,1)} %all_to_all.20.part_ref), custom_call_target="tpu_custom_call" | custom-call | tf_op jit(solution)/shard_map/merge/pallas_call | solution.py:171
  151.7 2.0 %collective-permute-start.22 = (bf16[256,256]{1,0:T(8,128)(2,1)}, bf16[256,256]{1,0:T(8,128)(2,1)S(1)}, u32[]{:S(2)}, u32[]{:S(2)}) collective-permute-start(bf16[256,256]{1,0:T(8,128)(2,1)} %merge.1.refs_0_), channel_id=1, source_target_pairs={{0,32},{16,48},{32,0},{48,16},{1,33},{17,49},{33,1},{49,17},{2,34}... | collective-permute-start | bytes 393224 | tf_op jit(solution)/shard_map/ppermute | solution.py:403
  153.7 2.3 %collective-permute-start.23 = (bf16[256,256]{1,0:T(8,128)(2,1)}, bf16[256,256]{1,0:T(8,128)(2,1)S(1)}, u32[]{:S(2)}, u32[]{:S(2)}) collective-permute-start(bf16[256,256]{1,0:T(8,128)(2,1)} %merge.1.refs_0_), channel_id=1, source_target_pairs={{0,48},{16,0},{32,16},{48,32},{1,49},{17,1},{33,17},{49,33},{2,50}... | collective-permute-start | bytes 393224 | tf_op jit(solution)/shard_map/ppermute | solution.py:403
  156.0 1.1 copy-done.2
  157.1 3.4 %weave_out.1.refs_4_ = bf16[1280,1024]{1,0:T(8,128)(2,1)} custom-call(s32[4]{0:T(128)} %pad_add_fusion.place_ref, bf16[640,1024]{1,0:T(8,128)(2,1)} %settle.1.refs_0_, bf16[640,1024]{1,0:T(8,128)(2,1)} %copy-done.2), custom_call_target="tpu_custom_call" | custom-call | tf_op jit(solution)/shard_map/weave_out/pallas_call | solution.py:366
  160.5 0.8 collective-permute-done.21.refs_1_
  162.0 0.7 copy-done.24
  162.6 3.8 %project.1 = bf16[16,16,1280]{2,1,0:T(8,128)(2,1)} custom-call(s32[4]{0:T(128)} %pad_add_fusion.place_ref, bf16[256,256]{1,0:T(8,128)(2,1)} %merge.1.refs_0_, bf16[256,256]{1,0:T(8,128)(2,1)} %copy-done.22, bf16[256,256]{1,0:T(8,128)(2,1)} %copy-done.23, bf16[256,256]{1,0:T(8,128)(2,1)} %copy-done.24, bf16[1280,1024]{1,0:T(8,128)(2,1)} %weave_out.1.refs_4_), custom_call_target="tpu_custom_call" | custom-call | tf_op jit(solution)/shard_map/project/pallas_call | solution.py:195
  166.4 19.6 %all_to_all.21.part_ref = bf16[16,16,1280]{2,1,0:T(8,128)(2,1)} all-to-all(bf16[16,16,1280]{2,1,0:T(8,128)(2,1)} %project.1), channel_id=1, replica_groups=mesh['tm'=2,'y'=4,'zl'=2,'x'=4,'c'=2] {'y','x'}, dimensions={0} | all-to-all | bytes 1310720 | tf_op jit(solution)/shard_map/all_to_all | solution.py:417
  186.0 1.8 finish.1
  (76 shorter events, 3.6 us)
Async XLA Ops:
  2.1 7.6 %copy-start.3 = (bf16[80,4096]{1,0:T(8,128)(2,1)S(1)}, bf16[80,4096]{1,0:T(8,128)(2,1)}, u32[]{:S(2)}) copy-start(bf16[80,4096]{1,0:T(8,128)(2,1)} %near_ref.1) | copy-start | bytes 1966084
  2.1 49.8 %all-to-all-start = ((bf16[32,16,1280]{2,1,0:T(8,128)(2,1)}), bf16[32,16,1280]{2,1,0:T(8,128)(2,1)S(1)}, u32[]{:S(2)}, u32[]{:S(2)}) async-start(bf16[32,16,1280]{2,1,0:T(8,128)(2,1)} %pack_tokens.1), calls=%async_computation | async-start | bytes 2621440 | tf_op jit(solution)/shard_map/all_to_all | solution.py:417
  9.7 2.2 %collective-permute-start = (bf16[80,4096]{1,0:T(8,128)(2,1)S(1)}, bf16[80,4096]{1,0:T(8,128)(2,1)S(1)}, u32[]{:S(2)}, u32[]{:S(2)}) collective-permute-start(bf16[80,4096]{1,0:T(8,128)(2,1)S(1)} %copy-done.3), channel_id=1, source_target_pairs={{0,1},{1,0},{2,3},{3,2},{4,5},{5,4},{6,7},{7,6},{8,9},{9,8},{10,11... | collective-permute-start | bytes 1966088 | tf_op jit(solution)/shard_map/ppermute | solution.py:413
  11.8 0.9 copy-start.4
  15.0 16.3 %collective-permute-start.1 = (bf16[2,80,512]{2,1,0:T(8,128)(2,1)}, bf16[2,80,512]{2,1,0:T(8,128)(2,1)S(1)}, u32[]{:S(2)}, u32[]{:S(2)}) collective-permute-start(bf16[2,80,512]{2,1,0:T(8,128)(2,1)} %get-tuple-element.39), channel_id=1, source_target_pairs={{0,2},{2,4},{4,6},{6,0},{1,3},{3,5},{5,7},{7,1},{8,10},{10,12},{12... | collective-permute-start | bytes 491528 | tf_op jit(solution)/shard_map/ppermute | solution.py:403
  16.8 18.5 %collective-permute-start.2 = (bf16[2,80,512]{2,1,0:T(8,128)(2,1)}, bf16[2,80,512]{2,1,0:T(8,128)(2,1)S(1)}, u32[]{:S(2)}, u32[]{:S(2)}) collective-permute-start(bf16[2,80,512]{2,1,0:T(8,128)(2,1)} %get-tuple-element.40), channel_id=1, source_target_pairs={{0,4},{2,6},{4,0},{6,2},{1,5},{3,7},{5,1},{7,3},{8,12},{10,14},{12... | collective-permute-start | bytes 491528 | tf_op jit(solution)/shard_map/ppermute | solution.py:403
  19.5 19.9 %collective-permute-start.3 = (bf16[2,80,512]{2,1,0:T(8,128)(2,1)}, bf16[2,80,512]{2,1,0:T(8,128)(2,1)S(1)}, u32[]{:S(2)}, u32[]{:S(2)}) collective-permute-start(bf16[2,80,512]{2,1,0:T(8,128)(2,1)} %get-tuple-element.41), channel_id=1, source_target_pairs={{0,6},{2,0},{4,2},{6,4},{1,7},{3,1},{5,3},{7,5},{8,14},{10,8},{12,... | collective-permute-start | bytes 491528 | tf_op jit(solution)/shard_map/ppermute | solution.py:403
  20.9 20.9 %collective-permute-start.4 = (bf16[2,80,512]{2,1,0:T(8,128)(2,1)}, bf16[2,80,512]{2,1,0:T(8,128)(2,1)S(1)}, u32[]{:S(2)}, u32[]{:S(2)}) collective-permute-start(bf16[2,80,512]{2,1,0:T(8,128)(2,1)} %get-tuple-element.38.refs_0_), channel_id=1, source_target_pairs={{0,8},{8,64},{64,72},{72,0},{1,9},{9,65},{65,73},{73,1},{2,10},{10... | collective-permute-start | bytes 491528 | tf_op jit(solution)/shard_map/ppermute | solution.py:399
  31.3 16.4 %copy-start.11 = (bf16[2,80,512]{2,1,0:T(8,128)(2,1)}, bf16[2,80,512]{2,1,0:T(8,128)(2,1)S(1)}, u32[]{:S(2)}) copy-start(bf16[2,80,512]{2,1,0:T(8,128)(2,1)S(1)} %collective-permute-done.1.refs_1_) | copy-start | bytes 491524
  31.3 12.6 %collective-permute-start.5 = (bf16[2,80,512]{2,1,0:T(8,128)(2,1)S(1)}, bf16[2,80,512]{2,1,0:T(8,128)(2,1)S(1)}, u32[]{:S(2)}, u32[]{:S(2)}) collective-permute-start(bf16[2,80,512]{2,1,0:T(8,128)(2,1)S(1)} %collective-permute-done.1.refs_1_), channel_id=1, source_target_pairs={{0,8},{8,64},{64,72},{72,0},{1,9},{9,65},{65,73},{73,1},{2,10},{10... | collective-permute-start | bytes 491528 | tf_op jit(solution)/shard_map/ppermute | solution.py:399
  35.3 12.4 %copy-start.12 = (bf16[2,80,512]{2,1,0:T(8,128)(2,1)}, bf16[2,80,512]{2,1,0:T(8,128)(2,1)S(1)}, u32[]{:S(2)}) copy-start(bf16[2,80,512]{2,1,0:T(8,128)(2,1)S(1)} %collective-permute-done.2.refs_2_) | copy-start | bytes 491524
  35.3 12.4 %collective-permute-start.6 = (bf16[2,80,512]{2,1,0:T(8,128)(2,1)S(1)}, bf16[2,80,512]{2,1,0:T(8,128)(2,1)S(1)}, u32[]{:S(2)}, u32[]{:S(2)}) collective-permute-start(bf16[2,80,512]{2,1,0:T(8,128)(2,1)S(1)} %collective-permute-done.2.refs_2_), channel_id=1, source_target_pairs={{0,72},{8,0},{64,8},{72,64},{1,73},{9,1},{65,9},{73,65},{2,74},{10... | collective-permute-start | bytes 491528 | tf_op jit(solution)/shard_map/ppermute | solution.py:399
  39.4 8.3 %copy-start.13 = (bf16[2,80,512]{2,1,0:T(8,128)(2,1)}, bf16[2,80,512]{2,1,0:T(8,128)(2,1)S(1)}, u32[]{:S(2)}) copy-start(bf16[2,80,512]{2,1,0:T(8,128)(2,1)S(1)} %collective-permute-done.3.refs_3_) | copy-start | bytes 491524
  39.4 8.4 %collective-permute-start.7 = (bf16[2,80,512]{2,1,0:T(8,128)(2,1)S(1)}, bf16[2,80,512]{2,1,0:T(8,128)(2,1)S(1)}, u32[]{:S(2)}, u32[]{:S(2)}) collective-permute-start(bf16[2,80,512]{2,1,0:T(8,128)(2,1)S(1)} %collective-permute-done.3.refs_3_), channel_id=1, source_target_pairs={{0,72},{8,0},{64,8},{72,64},{1,73},{9,1},{65,9},{73,65},{2,74},{10... | collective-permute-start | bytes 491528 | tf_op jit(solution)/shard_map/ppermute | solution.py:399
  41.8 14.7 %collective-permute-start.10 = (bf16[80,1024]{1,0:T(8,128)(2,1)}, bf16[80,1024]{1,0:T(8,128)(2,1)S(1)}, u32[]{:S(2)}, u32[]{:S(2)}) collective-permute-start(bf16[80,1024]{1,0:T(8,128)(2,1)} %get-tuple-element.52), channel_id=1, source_target_pairs={{0,6},{2,0},{4,2},{6,4},{1,7},{3,1},{5,3},{7,5},{8,14},{10,8},{12,... | collective-permute-start | bytes 491528 | tf_op jit(solution)/shard_map/ppermute | solution.py:403
  41.9 5.8 %copy-start.14 = (bf16[2,80,512]{2,1,0:T(8,128)(2,1)}, bf16[2,80,512]{2,1,0:T(8,128)(2,1)S(1)}, u32[]{:S(2)}) copy-start(bf16[2,80,512]{2,1,0:T(8,128)(2,1)S(1)} %collective-permute-done.4.refs_4_) | copy-start | bytes 491524
  41.9 14.7 %collective-permute-start.8 = (bf16[80,1024]{1,0:T(8,128)(2,1)}, bf16[80,1024]{1,0:T(8,128)(2,1)S(1)}, u32[]{:S(2)}, u32[]{:S(2)}) collective-permute-start(bf16[80,1024]{1,0:T(8,128)(2,1)} %get-tuple-element.50), channel_id=1, source_target_pairs={{0,2},{2,4},{4,6},{6,0},{1,3},{3,5},{5,7},{7,1},{8,10},{10,12},{12... | collective-permute-start | bytes 491528 | tf_op jit(solution)/shard_map/ppermute | solution.py:403
  43.9 3.8 %copy-start.15 = (bf16[2,80,512]{2,1,0:T(8,128)(2,1)}, bf16[2,80,512]{2,1,0:T(8,128)(2,1)S(1)}, u32[]{:S(2)}) copy-start(bf16[2,80,512]{2,1,0:T(8,128)(2,1)S(1)} %collective-permute-done.5.refs_5_) | copy-start | bytes 491524
  43.9 12.7 %collective-permute-start.9 = (bf16[80,1024]{1,0:T(8,128)(2,1)}, bf16[80,1024]{1,0:T(8,128)(2,1)S(1)}, u32[]{:S(2)}, u32[]{:S(2)}) collective-permute-start(bf16[80,1024]{1,0:T(8,128)(2,1)} %get-tuple-element.51), channel_id=1, source_target_pairs={{0,4},{2,6},{4,0},{6,2},{1,5},{3,7},{5,1},{7,3},{8,12},{10,14},{12... | collective-permute-start | bytes 491528 | tf_op jit(solution)/shard_map/ppermute | solution.py:403
  51.9 1.1 copy-start
  56.5 56.3 %copy-start.8 = (bf16[80,1024]{1,0:T(8,128)(2,1)}, bf16[80,1024]{1,0:T(8,128)(2,1)S(1)}, u32[]{:S(2)}) copy-start(bf16[80,1024]{1,0:T(8,128)(2,1)S(1)} %collective-permute-done.10.refs_3_) | copy-start | bytes 491524
  56.5 50.5 %copy-start.9 = (bf16[80,1024]{1,0:T(8,128)(2,1)}, bf16[80,1024]{1,0:T(8,128)(2,1)S(1)}, u32[]{:S(2)}) copy-start(bf16[80,1024]{1,0:T(8,128)(2,1)S(1)} %collective-permute-done.8.refs_1_) | copy-start | bytes 491524
  56.5 56.3 %copy-start.10 = (bf16[80,1024]{1,0:T(8,128)(2,1)}, bf16[80,1024]{1,0:T(8,128)(2,1)S(1)}, u32[]{:S(2)}) copy-start(bf16[80,1024]{1,0:T(8,128)(2,1)S(1)} %collective-permute-done.9.refs_2_) | copy-start | bytes 491524
  56.6 9.2 %copy-start.26 = (f32[512,128]{1,0:T(8,128)S(1)}, f32[512,128]{1,0:T(8,128)}, u32[]{:S(2)}) copy-start(f32[512,128]{1,0:T(8,128)} %get-tuple-element.59) | copy-start | bytes 786436
  56.6 11.9 %copy-start.25 = (f32[512,128]{1,0:T(8,128)S(1)}, f32[512,128]{1,0:T(8,128)}, u32[]{:S(2)}) copy-start(f32[512,128]{1,0:T(8,128)} %get-tuple-element.60) | copy-start | bytes 786436
  56.6 45.4 %copy-start.6 = (f32[512,128]{1,0:T(8,128)S(1)}, f32[512,128]{1,0:T(8,128)}, u32[]{:S(2)}) copy-start(f32[512,128]{1,0:T(8,128)} %get-tuple-element.57) | copy-start | bytes 786436
  56.6 50.5 %copy-start.7 = (bf16[80,1024]{1,0:T(8,128)(2,1)S(1)}, bf16[80,1024]{1,0:T(8,128)(2,1)}, u32[]{:S(2)}) copy-start(bf16[80,1024]{1,0:T(8,128)(2,1)} %get-tuple-element.63.refs_0_) | copy-start | bytes 491524
  56.6 57.7 %all-to-all-start.1 = ((bf16[32,256,128]{2,1,0:T(8,128)(2,1)}), bf16[32,256,128]{2,1,0:T(8,128)(2,1)S(1)}, u32[]{:S(2)}, u32[]{:S(2)}) async-start(bf16[32,256,128]{2,1,0:T(8,128)(2,1)} %pack_cache.1), calls=%async_computation.1 | async-start | bytes 4194304 | tf_op jit(solution)/shard_map/all_to_all | solution.py:417
  63.9 32.5 %collective-permute-start.15 = (f32[512,128]{1,0:T(8,128)}, f32[512,128]{1,0:T(8,128)S(1)}, u32[]{:S(2)}, u32[]{:S(2)}) collective-permute-start(f32[512,128]{1,0:T(8,128)} %get-tuple-element.58), channel_id=1, source_target_pairs={{0,16},{16,32},{32,48},{48,0},{1,17},{17,33},{33,49},{49,1},{2,18}... | collective-permute-start | bytes 786440 | tf_op jit(solution)/shard_map/ppermute | solution.py:403
  65.8 36.2 %collective-permute-start.16 = (f32[512,128]{1,0:T(8,128)S(1)}, f32[512,128]{1,0:T(8,128)S(1)}, u32[]{:S(2)}, u32[]{:S(2)}) collective-permute-start(f32[512,128]{1,0:T(8,128)S(1)} %copy-done.26), channel_id=1, source_target_pairs={{0,32},{16,48},{32,0},{48,16},{1,33},{17,49},{33,1},{49,17},{2,34}... | collective-permute-start | bytes 786440 | tf_op jit(solution)/shard_map/ppermute | solution.py:403
  68.5 33.5 %collective-permute-start.17 = (f32[512,128]{1,0:T(8,128)S(1)}, f32[512,128]{1,0:T(8,128)S(1)}, u32[]{:S(2)}, u32[]{:S(2)}) collective-permute-start(f32[512,128]{1,0:T(8,128)S(1)} %copy-done.25), channel_id=1, source_target_pairs={{0,48},{16,0},{32,16},{48,32},{1,49},{17,1},{33,17},{49,33},{2,50}... | collective-permute-start | bytes 786440 | tf_op jit(solution)/shard_map/ppermute | solution.py:403
  102.7 10.1 %collective-permute-start.18 = (bf16[512,128]{1,0:T(8,128)(2,1)}, bf16[512,128]{1,0:T(8,128)(2,1)}, u32[]{:S(2)}, u32[]{:S(2)}) collective-permute-start(bf16[512,128]{1,0:T(8,128)(2,1)} %add_convert_fusion.refs_0_), channel_id=1, source_target_pairs={{0,8},{8,64},{64,72},{72,0},{1,9},{9,65},{65,73},{73,1},{2,10},{10... | collective-permute-start | bytes 393224 | tf_op jit(solution)/shard_map/ppermute | solution.py:399
  104.4 8.5 %collective-permute-start.19 = (bf16[512,128]{1,0:T(8,128)(2,1)}, bf16[512,128]{1,0:T(8,128)(2,1)}, u32[]{:S(2)}, u32[]{:S(2)}) collective-permute-start(bf16[512,128]{1,0:T(8,128)(2,1)} %add_convert_fusion.refs_0_), channel_id=1, source_target_pairs={{0,64},{8,72},{64,0},{72,8},{1,65},{9,73},{65,1},{73,9},{2,66},{10... | collective-permute-start | bytes 393224 | tf_op jit(solution)/shard_map/ppermute | solution.py:399
  104.4 9.9 %collective-permute-start.20 = (bf16[512,128]{1,0:T(8,128)(2,1)}, bf16[512,128]{1,0:T(8,128)(2,1)}, u32[]{:S(2)}, u32[]{:S(2)}) collective-permute-start(bf16[512,128]{1,0:T(8,128)(2,1)} %add_convert_fusion.refs_0_), channel_id=1, source_target_pairs={{0,72},{8,0},{64,8},{72,64},{1,73},{9,1},{65,9},{73,65},{2,74},{10... | collective-permute-start | bytes 393224 | tf_op jit(solution)/shard_map/ppermute | solution.py:399
  107.0 23.9 %collective-permute-start.11 = (bf16[80,1024]{1,0:T(8,128)(2,1)S(1)}, bf16[80,1024]{1,0:T(8,128)(2,1)S(1)}, u32[]{:S(2)}, u32[]{:S(2)}) collective-permute-start(bf16[80,1024]{1,0:T(8,128)(2,1)S(1)} %copy-done.7), channel_id=1, source_target_pairs={{0,8},{8,64},{64,72},{72,0},{1,9},{9,65},{65,73},{73,1},{2,10},{10... | collective-permute-start | bytes 491528 | tf_op jit(solution)/shard_map/ppermute | solution.py:399
  107.1 23.9 %collective-permute-start.12 = (bf16[80,1024]{1,0:T(8,128)(2,1)S(1)}, bf16[80,1024]{1,0:T(8,128)(2,1)S(1)}, u32[]{:S(2)}, u32[]{:S(2)}) collective-permute-start(bf16[80,1024]{1,0:T(8,128)(2,1)S(1)} %collective-permute-done.8.refs_1_), channel_id=1, source_target_pairs={{0,8},{8,64},{64,72},{72,0},{1,9},{9,65},{65,73},{73,1},{2,10},{10... | collective-permute-start | bytes 491528 | tf_op jit(solution)/shard_map/ppermute | solution.py:399
  112.8 18.1 %collective-permute-start.13 = (bf16[80,1024]{1,0:T(8,128)(2,1)S(1)}, bf16[80,1024]{1,0:T(8,128)(2,1)S(1)}, u32[]{:S(2)}, u32[]{:S(2)}) collective-permute-start(bf16[80,1024]{1,0:T(8,128)(2,1)S(1)} %collective-permute-done.9.refs_2_), channel_id=1, source_target_pairs={{0,72},{8,0},{64,8},{72,64},{1,73},{9,1},{65,9},{73,65},{2,74},{10... | collective-permute-start | bytes 491528 | tf_op jit(solution)/shard_map/ppermute | solution.py:399
  112.9 18.1 %collective-permute-start.14 = (bf16[80,1024]{1,0:T(8,128)(2,1)S(1)}, bf16[80,1024]{1,0:T(8,128)(2,1)S(1)}, u32[]{:S(2)}, u32[]{:S(2)}) collective-permute-start(bf16[80,1024]{1,0:T(8,128)(2,1)S(1)} %collective-permute-done.10.refs_3_), channel_id=1, source_target_pairs={{0,72},{8,0},{64,8},{72,64},{1,73},{9,1},{65,9},{73,65},{2,74},{10... | collective-permute-start | bytes 491528 | tf_op jit(solution)/shard_map/ppermute | solution.py:399
  114.3 1.3 copy-start.1
  130.9 4.0 %copy-start.5 = (bf16[8,272,128]{2,1,0:T(8,128)(2,1)S(1)}, bf16[8,272,128]{2,1,0:T(8,128)(2,1)}, u32[]{:S(2)}) copy-start(bf16[8,272,128]{2,1,0:T(8,128)(2,1)} %attend.1) | copy-start | bytes 1671172
  131.0 0.7 copy-start.17
  131.0 0.7 copy-start.19
  135.0 21.1 %collective-permute-start.24 = (bf16[640,1024]{1,0:T(8,128)(2,1)}, bf16[640,1024]{1,0:T(8,128)(2,1)S(1)}, u32[]{:S(2)}, u32[]{:S(2)}) collective-permute-start(bf16[640,1024]{1,0:T(8,128)(2,1)} %settle.1.refs_0_), channel_id=1, source_target_pairs={{0,1},{1,0},{2,3},{3,2},{4,5},{5,4},{6,7},{7,6},{8,9},{9,8},{10,11... | collective-permute-start | bytes 3932168 | tf_op jit(solution)/shard_map/ppermute | solution.py:413
  151.7 9.6 %collective-permute-start.21 = (bf16[256,256]{1,0:T(8,128)(2,1)}, bf16[256,256]{1,0:T(8,128)(2,1)S(1)}, u32[]{:S(2)}, u32[]{:S(2)}) collective-permute-start(bf16[256,256]{1,0:T(8,128)(2,1)} %merge.1.refs_0_), channel_id=1, source_target_pairs={{0,16},{16,32},{32,48},{48,0},{1,17},{17,33},{33,49},{49,1},{2,18}... | collective-permute-start | bytes 393224 | tf_op jit(solution)/shard_map/ppermute | solution.py:403
  151.7 9.6 %collective-permute-start.22 = (bf16[256,256]{1,0:T(8,128)(2,1)}, bf16[256,256]{1,0:T(8,128)(2,1)S(1)}, u32[]{:S(2)}, u32[]{:S(2)}) collective-permute-start(bf16[256,256]{1,0:T(8,128)(2,1)} %merge.1.refs_0_), channel_id=1, source_target_pairs={{0,32},{16,48},{32,0},{48,16},{1,33},{17,49},{33,1},{49,17},{2,34}... | collective-permute-start | bytes 393224 | tf_op jit(solution)/shard_map/ppermute | solution.py:403
  153.7 8.2 %collective-permute-start.23 = (bf16[256,256]{1,0:T(8,128)(2,1)}, bf16[256,256]{1,0:T(8,128)(2,1)S(1)}, u32[]{:S(2)}, u32[]{:S(2)}) collective-permute-start(bf16[256,256]{1,0:T(8,128)(2,1)} %merge.1.refs_0_), channel_id=1, source_target_pairs={{0,48},{16,0},{32,16},{48,32},{1,49},{17,1},{33,17},{49,33},{2,50}... | collective-permute-start | bytes 393224 | tf_op jit(solution)/shard_map/ppermute | solution.py:403
  156.0 1.1 copy-start.2
  161.3 0.7 copy-start.23
  (6 other events, 4.0 us)
